TPU v7x, 32 devices: a 4x4x1 block of a 4x4x8 slice. The times are simulated.
32 devices in a mesh: dp: 1 (over z), ep: 32 (over y, x, core).
Axes of the slice: x: 4, y: 4, z: 1, core: 2. Of those that a mesh axis runs over, the one named last changes fastest.
The devices are a block of a 4x4x8 slice.
Arguments:
- resid_in: bfloat16 [2, 32, 1024, 1024], P(None, ('dp', 'ep'))
- expert_idx: int32 [2, 32, 1024, 8], P(None, ('dp', 'ep'))
- expert_slot: int32 [2, 32, 1024, 8], P(None, ('dp', 'ep'))
- w_query: bfloat16 [1024, 16, 64], replicated
- w_key: bfloat16 [1024, 8, 64], replicated
- w_value: bfloat16 [1024, 8, 64], replicated
- w_out: bfloat16 [16, 64, 1024], replicated
- w_gate: bfloat16 [1024, 4096], replicated
- w_up: bfloat16 [1024, 4096], replicated
- w_down: bfloat16 [4096, 1024], replicated
- w_router: bfloat16 [1024, 32], replicated
- norm_attn: bfloat16 [1024], replicated
- norm_ffn: bfloat16 [1024], replicated
- norm_moe: bfloat16 [1024], replicated
- expert_gate: bfloat16 [32, 1024, 512], P('ep')
- expert_up: bfloat16 [32, 1024, 512], P('ep')
- expert_down: bfloat16 [32, 512, 1024], P('ep')
Outputs:
- output: bfloat16 [2, 32, 1024, 1024], P(None, ('dp', 'ep'))
All inputs are finite; a program needn't handle non-finite values.
Results may differ from a plain program's by a relative error of at most 0.010065.
Values are sent between devices in bfloat16 or wider.
A program may use at most 768 MiB of HBM per device.

v0:
```python
import jax
import jax.numpy as jnp
from jax import lax
from jax.sharding import PartitionSpec as P, NamedSharding

EPS = 1e-6
ROPE_BASE = 10000.0
CAP_FACTOR = 2


def rms_norm(values, scale):
    widened = values.astype(jnp.float32)
    mean_sq = jnp.mean(widened * widened, axis=-1, keepdims=True)
    return (widened * lax.rsqrt(mean_sq + EPS) * scale.astype(jnp.float32)).astype(jnp.bfloat16)


def rotary(values):
    seq_len = values.shape[-3]
    head_dim = values.shape[-1]
    half_dim = head_dim // 2
    freqs = ROPE_BASE ** (-jnp.arange(half_dim, dtype=jnp.float32) * 2.0 / head_dim)
    angles = jnp.arange(seq_len, dtype=jnp.float32)[:, None] * freqs[None, :]
    cosine = jnp.cos(angles)[:, None, :]
    sine = jnp.sin(angles)[:, None, :]
    first = values[..., :half_dim]
    second = values[..., half_dim:]
    return jnp.concatenate([first * cosine - second * sine, second * cosine + first * sine], axis=-1)


def dense_branch(resid, norm_attn, w_query, w_key, w_value, w_out, norm_ffn, w_gate, w_up, w_down):
    batch, seq_len = resid.shape[0], resid.shape[1]
    heads, head_dim = w_query.shape[1], w_query.shape[2]
    kv_heads = w_key.shape[1]
    normed = rms_norm(resid, norm_attn)
    queries = rotary(jnp.einsum('bsd,dhe->bshe', normed, w_query, preferred_element_type=jnp.float32)).astype(jnp.bfloat16)
    keys_rot = rotary(jnp.einsum('bsd,dhe->bshe', normed, w_key, preferred_element_type=jnp.float32)).astype(jnp.bfloat16)
    values_in = jnp.einsum('bsd,dhe->bshe', normed, w_value, preferred_element_type=jnp.float32).astype(jnp.bfloat16)
    grouped = queries.reshape(batch, seq_len, kv_heads, heads // kv_heads, head_dim)
    scores = jnp.einsum('bqgre,bkge->bgrqk', grouped, keys_rot, preferred_element_type=jnp.float32) * (head_dim ** -0.5)
    causal = jnp.arange(seq_len)[:, None] >= jnp.arange(seq_len)[None, :]
    probs = jax.nn.softmax(jnp.where(causal, scores, -1e30), axis=-1).astype(jnp.bfloat16)
    attended = jnp.einsum('bgrqk,bkge->bqgre', probs, values_in, preferred_element_type=jnp.float32).astype(jnp.bfloat16)
    attn_out = jnp.einsum('bshe,hed->bsd', attended.reshape(batch, seq_len, heads, head_dim), w_out, preferred_element_type=jnp.float32)
    after_attn = (resid.astype(jnp.float32) + attn_out).astype(jnp.bfloat16)
    normed_ffn = rms_norm(after_attn, norm_ffn)
    gate_act = jnp.einsum('bsd,df->bsf', normed_ffn, w_gate, preferred_element_type=jnp.float32)
    up_act = jnp.einsum('bsd,df->bsf', normed_ffn, w_up, preferred_element_type=jnp.float32)
    hidden = (jax.nn.silu(gate_act) * up_act).astype(jnp.bfloat16)
    down_act = jnp.einsum('bsf,fd->bsd', hidden, w_down, preferred_element_type=jnp.float32)
    return after_attn.astype(jnp.float32) + down_act


def route(tokens_in, norm_moe, w_router, route_ids):
    normed = rms_norm(tokens_in, norm_moe)
    logits = jnp.dot(normed, w_router, preferred_element_type=jnp.float32)
    picked = jnp.take_along_axis(logits, route_ids, axis=1)
    return normed, jax.nn.softmax(picked, axis=-1)


def expert_ffn(rows_in, expert_gate, expert_up, expert_down):
    gate_act = jnp.einsum('lrd,ldf->lrf', rows_in, expert_gate, preferred_element_type=jnp.float32)
    up_act = jnp.einsum('lrd,ldf->lrf', rows_in, expert_up, preferred_element_type=jnp.float32)
    hidden = (jax.nn.silu(gate_act) * up_act).astype(jnp.bfloat16)
    return jnp.einsum('lrf,lfd->lrd', hidden, expert_down, preferred_element_type=jnp.float32).astype(jnp.bfloat16)


def solution(mesh):
    group_size = mesh.shape['ep']
    tok_spec = P(None, ('dp', 'ep'), None, None)
    rep_one = P(None)
    rep_two = P(None, None)
    rep_three = P(None, None, None)
    expert_spec = P('ep', None, None)

    def local_program(resid_in, expert_idx, expert_slot, w_query, w_key, w_value, w_out, w_gate, w_up, w_down, w_router, norm_attn, norm_ffn, norm_moe, expert_gate, expert_up, expert_down):
        micro_count, seqs, seq_len, width = resid_in.shape
        tokens = seqs * seq_len
        choices = expert_idx.shape[-1]
        local_experts = expert_gate.shape[0]
        capacity = CAP_FACTOR * tokens * choices // (local_experts * group_size)
        buf_rows = local_experts * group_size * capacity
        token_of_copy = jnp.broadcast_to(jnp.arange(tokens, dtype=jnp.int32)[:, None], (tokens, choices)).reshape(-1)
        outputs = []
        for micro in range(micro_count):
            resid = resid_in[micro]
            route_ids = expert_idx[micro].reshape(tokens, choices)
            route_slots = expert_slot[micro].reshape(tokens, choices)
            normed, gates = route(resid.reshape(tokens, width), norm_moe, w_router, route_ids)
            buf_pos = ((route_ids % local_experts) * group_size + route_ids // local_experts) * capacity + route_slots
            source_row = jnp.full((buf_rows,), tokens, jnp.int32).at[buf_pos.reshape(-1)].set(token_of_copy)
            send_buf = jnp.take(normed, source_row, axis=0, mode='fill', fill_value=0).reshape(local_experts, group_size, capacity, width)
            received = lax.all_to_all(send_buf, 'ep', 1, 1, tiled=True)
            expert_out = expert_ffn(received.reshape(local_experts, group_size * capacity, width), expert_gate, expert_up, expert_down)
            returned = lax.all_to_all(expert_out.reshape(local_experts, group_size, capacity, width), 'ep', 1, 1, tiled=True)
            per_copy = jnp.take(returned.reshape(buf_rows, width), buf_pos, axis=0)
            moe_out = jnp.sum(gates[:, :, None] * per_copy.astype(jnp.float32), axis=1)
            dense_out = dense_branch(resid, norm_attn, w_query, w_key, w_value, w_out, norm_ffn, w_gate, w_up, w_down)
            outputs.append((dense_out + moe_out.reshape(seqs, seq_len, width)).astype(jnp.bfloat16))
        return jnp.stack(outputs)

    return jax.shard_map(local_program, mesh=mesh, in_specs=(tok_spec, tok_spec, tok_spec, rep_three, rep_three, rep_three, rep_three, rep_two, rep_two, rep_two, rep_two, rep_one, rep_one, rep_one, expert_spec, expert_spec, expert_spec), out_specs=tok_spec, check_vma=False)
```

profile of v0, /device:TPU:107, one launch (start us, length us, event | category | flops | bytes accessed | tf_op | source)
XLA Modules:
  0.0 2253.1 jit_solution(12775692081681951553)
XLA Ops:
  1.8 30.5 %scatter_custom_fusion = s32[16384]{0:T(1024)S(1)} fusion(s32[8192]{0:T(1024)S(1)} %bitcast.311, s32[8192]{0:T(1024)S(1)} %reshape.667, s32[]{:T(128)} %constant.115.clone.1), kind=kCustom, calls=%fused_computation.155 | custom fusion | bytes 65540 | tf_op jit(solution)/shard_map/scatter | solution.py:90
  59.0 81.9 %gather_fusion.1 = bf16[16384,1024]{1,0:T(8,128)(2,1)} fusion(bf16[1024,1024]{1,0:T(8,128)(2,1)} %copy.88, s32[16384]{0:T(1024)S(1)} %fusion.99), kind=kCustom, calls=%fused_computation.1.clone | custom fusion | bytes 67174400 | tf_op jit(solution)/shard_map/jit(_take)/gather | solution.py:91
  140.9 22.7 %broadcast_select_fusion.1 = bf16[16384,1024]{1,0:T(8,128)(2,1)} fusion(bf16[16384,1024]{1,0:T(8,128)(2,1)} %gather_fusion.1, pred[16384]{0:T(1024)(128)(4,1)S(1)} %compare_and_fusion.1), kind=kLoop, calls=%fused_computation.27 | loop fusion | flops 16777216 | bytes 67125248 | tf_op jit(solution)/shard_map/jit(_take)/select_n | solution.py:91
  163.6 7.7 all-to-all-start
  171.8 30.5 %scatter_custom_fusion.1 = s32[16384]{0:T(1024)S(1)} fusion(s32[8192]{0:T(1024)S(1)} %bitcast.312, s32[8192]{0:T(1024)S(1)} %reshape.667, s32[]{:T(128)} %constant.115.clone.1), kind=kCustom, calls=%fused_computation.153 | custom fusion | bytes 65540 | tf_op jit(solution)/shard_map/scatter | solution.py:90
  206.3 82.2 %gather_fusion.4 = bf16[16384,1024]{1,0:T(8,128)(2,1)} fusion(bf16[1024,1024]{1,0:T(8,128)(2,1)} %copy.104, s32[16384]{0:T(1024)S(1)} %fusion.100), kind=kCustom, calls=%fused_computation.4.clone | custom fusion | bytes 67174400 | tf_op jit(solution)/shard_map/jit(_take)/gather | solution.py:91
  288.5 22.7 %broadcast_select_fusion = bf16[16384,1024]{1,0:T(8,128)(2,1)} fusion(bf16[16384,1024]{1,0:T(8,128)(2,1)} %gather_fusion.4, pred[16384]{0:T(1024)(128)(4,1)S(1)} %compare_and_fusion), kind=kLoop, calls=%fused_computation.26 | loop fusion | flops 16777216 | bytes 67125248 | tf_op jit(solution)/shard_map/jit(_take)/select_n | solution.py:91
  311.2 315.5 %all-to-all-done = bf16[1,32,512,1024]{3,2,0,1:T(8,128)(2,1)} async-done(((bf16[1,32,512,1024]{3,2,0,1:T(8,128)(2,1)}), bf16[1,32,512,1024]{3,2,0,1:T(8,128)(2,1)}, u32[]{:S(2)}, u32[]{:S(2)}) %all-to-all-start) | async-done | bytes 33554464 | tf_op jit(solution)/shard_map/all_to_all | solution.py:92
  631.9 31.5 %fusion.89 = f32[16384,512]{1,0:T(8,128)} fusion(bf16[16384,1024]{1,0:T(8,128)(2,1)} %bitcast.32, bf16[1,1024,512]{2,1,0:T(8,128)(2,1)S(1)} %copy-done.33), kind=kOutput, calls=%fused_computation.116 | convolution fusion | flops 17179869184 | bytes 68157440 | tf_op jit(solution)/shard_map/lrd,ldf->lrf/dot_general | solution.py:61
  663.4 47.5 %convolution_convert_fusion.1 = bf16[16384,1024]{1,0:T(8,128)(2,1)} fusion(f32[16384,512]{1,0:T(8,128)} %fusion.89, bf16[16384,1024]{1,0:T(8,128)(2,1)} %bitcast.32, bf16[1,512,1024]{2,1,0:T(8,128)(2,1)} %param.39, bf16[1,1024,512]{2,1,0:T(8,128)(2,1)} %param.38), kind=kOutput, calls=%fused_computation.29 | convolution fusion | flops 34426847232 | bytes 102760448 | tf_op jit(solution)/shard_map/lrf,lfd->lrd/dot_general | solution.py:64
  710.9 375.3 %all-to-all-done.2 = bf16[1,32,512,1024]{3,2,0,1:T(8,128)(2,1)} async-done(((bf16[1,32,512,1024]{3,2,0,1:T(8,128)(2,1)}), bf16[1,32,512,1024]{3,2,0,1:T(8,128)(2,1)}, u32[]{:S(2)}, u32[]{:S(2)}) %all-to-all-start.2) | async-done | bytes 33554464 | tf_op jit(solution)/shard_map/all_to_all | solution.py:92
  1099.9 65.5 %gather_fusion.3 = f32[8192]{0:T(1024)S(1)} fusion(f32[1024,32]{0,1:T(8,128)S(1)} %fusion.135, s32[8192]{0:T(1024)S(1)} %reshape.699), kind=kCustom, calls=%fused_computation.3.clone | custom fusion | bytes 131072 | tf_op jit(solution)/shard_map/jit(take_along_axis)/gather | solution.py:56
  1168.6 65.5 %gather_fusion = f32[8192]{0:T(1024)S(1)} fusion(f32[1024,32]{0,1:T(8,128)S(1)} %fusion.134, s32[8192]{0:T(1024)S(1)} %copy-done.2), kind=kCustom, calls=%fused_computation.clone | custom fusion | bytes 131072 | tf_op jit(solution)/shard_map/jit(take_along_axis)/gather | solution.py:56
  1256.0 24.1 %fusion.2 = (f32[8,2,1024]{2,1,0:T(2,128)S(1)}, f32[8,1024,1024,2]{2,1,3,0:T(8,128)}) fusion(pred[1024,1024]{0,1:T(8,128)(4,1)S(1)} %iota_compare_fusion, bf16[1024,8,2,32]{0,3,2,1:T(8,128)(2,1)S(1)} %bitcast.310, bf16[1024,8,2,32]{0,3,2,1:T(8,128)(2,1)S(1)} %bitcast.309, bf16[1024,8,32]{0,2,1:T(8,128)(2,1)S(1)} %get-tuple-element.25, ...), kind=kOutput, calls=%fused_computation.16 | convolution fusion | flops 2204090368 | bytes 71368704 | tf_op jit(solution)/shard_map/bqgre,bkge->bgrqk/dot_general | solution.py:39
  1280.1 31.7 %fusion.87 = f32[16384,512]{1,0:T(8,128)} fusion(bf16[16384,1024]{1,0:T(8,128)(2,1)} %bitcast.73, bf16[1,1024,512]{2,1,0:T(8,128)(2,1)S(1)} %copy-done.34), kind=kOutput, calls=%fused_computation.114 | convolution fusion | flops 17179869184 | bytes 68157440 | tf_op jit(solution)/shard_map/lrd,ldf->lrf/dot_general | solution.py:61
  1311.8 46.9 %convolution_convert_fusion = bf16[16384,1024]{1,0:T(8,128)(2,1)} fusion(f32[16384,512]{1,0:T(8,128)} %fusion.87, bf16[16384,1024]{1,0:T(8,128)(2,1)} %bitcast.73, bf16[1,512,1024]{2,1,0:T(8,128)(2,1)S(1)} %copy-done.35, bf16[1,1024,512]{2,1,0:T(8,128)(2,1)S(1)} %copy-done.36), kind=kOutput, calls=%fused_computation.28 | convolution fusion | flops 34426847232 | bytes 102760448 | tf_op jit(solution)/shard_map/lrf,lfd->lrd/dot_general | solution.py:64
  1358.7 187.0 %all-to-all-done.1 = bf16[1,32,512,1024]{3,2,0,1:T(8,128)(2,1)} async-done(((bf16[1,32,512,1024]{3,2,0,1:T(8,128)(2,1)}), bf16[1,32,512,1024]{3,2,0,1:T(8,128)(2,1)}, u32[]{:S(2)}, u32[]{:S(2)}) %all-to-all-start.1) | async-done | bytes 33554464 | tf_op jit(solution)/shard_map/all_to_all | solution.py:94
  1551.0 50.8 %fusion = (f32[8,2,1024]{2,1,0:T(2,128)S(1)}, f32[8,2,1024]{2,1,0:T(2,128)S(1)}, f32[8,1024,1024,2]{2,1,3,0:T(8,128)}) fusion(f32[8,1024,1024,2]{2,1,3,0:T(8,128)} %get-tuple-element.45, f32[8,2,1024]{2,1,0:T(2,128)S(1)} %get-tuple-element.44, pred[1024,1024]{0,1:T(8,128)(4,1)S(1)} %iota_compare_fusion, bf16[1024,8,2,32]{0,3,2,1:T(8,128)(2,1)S(1)} %bitcast.307, ...), kind=kOutput, calls=%fused_computation.14 | convolution fusion | flops 2271182848 | bytes 138608640 | tf_op jit(solution)/shard_map/bqgre,bkge->bgrqk/dot_general | solution.py:39
  1601.8 27.0 %fusion.59 = bf16[8,64,2,1024]{3,1,2,0:T(8,128)(2,1)} fusion(f32[8,2,1024]{2,1,0:T(2,128)S(1)} %get-tuple-element.6, f32[8,2,1024]{2,1,0:T(2,128)S(1)} %get-tuple-element.44, f32[8,1024,1024,2]{2,1,3,0:T(8,128)} %get-tuple-element.45, pred[1024,1024]{0,1:T(8,128)(4,1)} %copy-done.7, f32[1024,8,64]{0,2,1:T(8,128)} %bitcast.319), kind=kOutput, calls=%fused_computation.97 | convolution fusion | flops 2232942592 | bytes 72482816 | tf_op jit(solution)/shard_map/bgrqk,bkge->bqgre/dot_general | solution.py:42
  1628.8 6.5 fusion.34
  1638.0 21.8 fusion.1
  1659.8 26.8 %fusion.62 = bf16[8,64,2,1024]{3,1,2,0:T(8,128)(2,1)} fusion(f32[8,2,1024]{2,1,0:T(2,128)S(1)} %fusion.1, f32[8,2,1024]{2,1,0:T(2,128)S(1)} %get-tuple-element.8, f32[8,1024,1024,2]{2,1,3,0:T(8,128)} %get-tuple-element.46, pred[1024,1024]{0,1:T(8,128)(4,1)S(1)} %copy-done.8, f32[1024,8,64]{0,2,1:T(8,128)} %bitcast.322), kind=kOutput, calls=%fused_computation.98 | convolution fusion | flops 2232942592 | bytes 72482816 | tf_op jit(solution)/shard_map/bgrqk,bkge->bqgre/dot_general | solution.py:42
  1691.8 16.2 fusion.54
  1708.0 12.1 fusion.67
  1720.1 150.1 %gather_fusion.2 = bf16[8192,1024]{1,0:T(8,128)(2,1)} fusion(bf16[16384,1024]{1,0:T(8,128)(2,1)} %bitcast.38, s32[8192]{0:T(1024)S(1)} %broadcast_clamp_fusion.1), kind=kCustom, calls=%fused_computation.2.clone | custom fusion | bytes 33587200 | tf_op jit(solution)/shard_map/jit(_take)/gather | solution.py:95
  1870.2 18.6 multiply_reduce_fusion.1
  1894.2 111.3 %all-to-all-done.3 = bf16[1,32,512,1024]{3,2,0,1:T(8,128)(2,1)} async-done(((bf16[1,32,512,1024]{3,2,0,1:T(8,128)(2,1)}), bf16[1,32,512,1024]{3,2,0,1:T(8,128)(2,1)}, u32[]{:S(2)}, u32[]{:S(2)}) %all-to-all-start.3) | async-done | bytes 33554464 | tf_op jit(solution)/shard_map/all_to_all | solution.py:94
  2005.5 150.2 %gather_fusion.5 = bf16[8192,1024]{1,0:T(8,128)(2,1)} fusion(bf16[16384,1024]{1,0:T(8,128)(2,1)} %bitcast.76, s32[8192]{0:T(1024)S(1)} %broadcast_clamp_fusion), kind=kCustom, calls=%fused_computation.5.clone | custom fusion | bytes 33587200 | tf_op jit(solution)/shard_map/jit(_take)/gather | solution.py:95
  2155.7 18.7 multiply_reduce_fusion
  2179.8 30.9 %fusion.69 = bf16[1,1,1024,1024]{2,3,1,0:T(8,128)(2,1)} fusion(f32[1024,1024]{0,1:T(8,128)} %copy.108, bf16[4096,1024]{1,0:T(8,128)(2,1)} %param.32, f32[1024,4096]{1,0:T(8,128)} %fusion.54, bf16[1024,4096]{1,0:T(8,128)(2,1)} %param.31, bf16[1024,1024]{0,1:T(8,128)(2,1)} %copy-done.40, f32[1024]{0:T(1024)S(1)} %add_rsqrt_fusion.1, f32[1024]{0:T(1024)S(1)} %copy-done.23), kind=kOutput, calls=%fused_computation.100 | convolution fusion | flops 17213423616 | bytes 41951232 | tf_op jit(solution)/shard_map/bsf,fd->bsd/dot_general | solution.py:49
  2210.8 31.2 %fusion.72 = bf16[1,1,1024,1024]{2,3,1,0:T(8,128)(2,1)} fusion(f32[1024,1024]{0,1:T(8,128)} %copy.92, bf16[4096,1024]{1,0:T(8,128)(2,1)} %param.32, f32[1024,4096]{1,0:T(8,128)} %fusion.67, bf16[1024,4096]{1,0:T(8,128)(2,1)} %param.31, bf16[1024,1024]{0,1:T(8,128)(2,1)} %get-tuple-element.50, f32[1024]{0:T(1024)S(1)} %copy-done.23, f32[1024]{0:T(1024)S(1)} %copy-done.29), kind=kOutput, calls=%fused_computation.101 | convolution fusion | flops 17213423616 | bytes 41951232 | tf_op jit(solution)/shard_map/bsf,fd->bsd/dot_general | solution.py:49
  2246.7 6.2 copy.109
  (161 shorter events, 105.1 us)
Async XLA Ops:
  0.0 1248.2 %copy-start = (bf16[1024,16,64]{0,2,1:T(8,128)(2,1)S(1)}, bf16[1024,16,64]{0,2,1:T(8,128)(2,1)}, u32[]{:S(2)}) copy-start(bf16[1024,16,64]{0,2,1:T(8,128)(2,1)} %param.26) | copy-start | bytes 6291460
  163.6 463.1 %all-to-all-start = ((bf16[1,32,512,1024]{3,2,0,1:T(8,128)(2,1)}), bf16[1,32,512,1024]{3,2,0,1:T(8,128)(2,1)}, u32[]{:S(2)}, u32[]{:S(2)}) async-start(bf16[1,32,512,1024]{3,2,0,1:T(8,128)(2,1)} %bitcast.299), calls=%async_computation | async-start | bytes 67108864 | tf_op jit(solution)/shard_map/all_to_all | solution.py:92
  626.7 459.5 %all-to-all-start.2 = ((bf16[1,32,512,1024]{3,2,0,1:T(8,128)(2,1)}), bf16[1,32,512,1024]{3,2,0,1:T(8,128)(2,1)}, u32[]{:S(2)}, u32[]{:S(2)}) async-start(bf16[1,32,512,1024]{3,2,0,1:T(8,128)(2,1)} %bitcast.300), calls=%async_computation.2 | async-start | bytes 67108864 | tf_op jit(solution)/shard_map/all_to_all | solution.py:92
  1086.2 6.2 copy-start.20
  1086.2 459.6 %all-to-all-start.1 = ((bf16[1,32,512,1024]{3,2,0,1:T(8,128)(2,1)}), bf16[1,32,512,1024]{3,2,0,1:T(8,128)(2,1)}, u32[]{:S(2)}, u32[]{:S(2)}) async-start(bf16[1,32,512,1024]{3,2,0,1:T(8,128)(2,1)} %bitcast.301), calls=%async_computation.1 | async-start | bytes 67108864 | tf_op jit(solution)/shard_map/all_to_all | solution.py:94
  1091.2 6.6 copy-start.18
  1099.9 66.6 %copy-start.19 = (bf16[1024,32]{0,1:T(8,128)(2,1)S(1)}, bf16[1024,32]{0,1:T(8,128)(2,1)}, u32[]{:S(2)}) copy-start(bf16[1024,32]{0,1:T(8,128)(2,1)} %param.33) | copy-start | bytes 196612
  1168.6 66.0 %copy-start.10 = (s32[2,1,1024,8]{2,3,1,0:T(8,128)S(1)}, s32[2,1,1024,8]{2,3,1,0:T(8,128)}, u32[]{:S(2)}) copy-start(s32[2,1,1024,8]{2,3,1,0:T(8,128)} %param.24) | copy-start | bytes 196612
  1168.6 66.0 %copy-start.17 = (f32[1024,8]{0,1:T(8,128)S(1)}, f32[1024,8]{0,1:T(8,128)}, u32[]{:S(2)}) copy-start(f32[1024,8]{0,1:T(8,128)} %copy.100) | copy-start | bytes 98308
  1234.1 6.7 copy-start.24
  1237.2 313.8 %copy-start.7 = (pred[1024,1024]{0,1:T(8,128)(4,1)}, pred[1024,1024]{0,1:T(8,128)(4,1)S(1)}, u32[]{:S(2)}) copy-start(pred[1024,1024]{0,1:T(8,128)(4,1)S(1)} %iota_compare_fusion) | copy-start | bytes 3145732
  1240.3 10.4 copy-start.26
  1256.0 24.1 %copy-start.34 = (bf16[1,1024,512]{2,1,0:T(8,128)(2,1)S(1)}, bf16[1,1024,512]{2,1,0:T(8,128)(2,1)}, u32[]{:S(2)}) copy-start(bf16[1,1024,512]{2,1,0:T(8,128)(2,1)} %param.37) | copy-start | bytes 3145732
  1280.1 31.7 %copy-start.35 = (bf16[1,512,1024]{2,1,0:T(8,128)(2,1)S(1)}, bf16[1,512,1024]{2,1,0:T(8,128)(2,1)}, u32[]{:S(2)}) copy-start(bf16[1,512,1024]{2,1,0:T(8,128)(2,1)} %param.39) | copy-start | bytes 3145732
  1280.1 31.7 %copy-start.36 = (bf16[1,1024,512]{2,1,0:T(8,128)(2,1)S(1)}, bf16[1,1024,512]{2,1,0:T(8,128)(2,1)}, u32[]{:S(2)}) copy-start(bf16[1,1024,512]{2,1,0:T(8,128)(2,1)} %param.38) | copy-start | bytes 3145732
  1545.8 459.7 %all-to-all-start.3 = ((bf16[1,32,512,1024]{3,2,0,1:T(8,128)(2,1)}), bf16[1,32,512,1024]{3,2,0,1:T(8,128)(2,1)}, u32[]{:S(2)}, u32[]{:S(2)}) async-start(bf16[1,32,512,1024]{3,2,0,1:T(8,128)(2,1)} %bitcast.302), calls=%async_computation.3 | async-start | bytes 67108864 | tf_op jit(solution)/shard_map/all_to_all | solution.py:94
  1601.8 27.0 %copy-start.6 = (bf16[1,1,1024,1024]{2,3,1,0:T(8,128)(2,1)S(1)}, bf16[1,1,1024,1024]{2,3,1,0:T(8,128)(2,1)}, u32[]{:S(2)}) copy-start(bf16[1,1,1024,1024]{2,3,1,0:T(8,128)(2,1)} %copy.124) | copy-start | bytes 6291460
  1628.8 6.5 copy-start.4
  1628.8 6.5 copy-start.25
  1628.8 6.5 copy-start.27
  1628.8 6.5 copy-start.38
  1635.3 72.7 %copy-start.28 = (f32[1024]{0:T(1024)}, f32[1024]{0:T(1024)S(1)}, u32[]{:S(2)}) copy-start(f32[1024]{0:T(1024)S(1)} %add_rsqrt_fusion.4) | copy-start | bytes 12292
  1686.6 21.4 slice-start
  1691.7 16.3 copy-start.40
  1691.8 16.2 slice-start.1
  1691.8 16.2 copy-start.39
  1720.1 150.1 %copy-start.12 = (f32[1024,8]{1,0:T(8,128)S(1)}, f32[1024,8]{1,0:T(8,128)}, u32[]{:S(2)}) copy-start(f32[1024,8]{1,0:T(8,128)} %copy.85) | copy-start | bytes 98308
  1720.1 150.1 %copy-start.16 = (pred[1024,8]{1,0:T(8,128)(4,1)S(1)}, pred[1024,8]{1,0:T(8,128)(4,1)}, u32[]{:S(2)}) copy-start(pred[1024,8]{1,0:T(8,128)(4,1)} %copy.86) | copy-start | bytes 24580
  2005.5 150.2 %copy-start.11 = (f32[1024,8]{1,0:T(8,128)S(1)}, f32[1024,8]{1,0:T(8,128)}, u32[]{:S(2)}) copy-start(f32[1024,8]{1,0:T(8,128)} %copy.101) | copy-start | bytes 98308
  2005.5 150.2 %copy-start.15 = (pred[1024,8]{1,0:T(8,128)(4,1)S(1)}, pred[1024,8]{1,0:T(8,128)(4,1)}, u32[]{:S(2)}) copy-start(pred[1024,8]{1,0:T(8,128)(4,1)} %copy.102) | copy-start | bytes 24580
  2179.8 31.0 %copy-start.29 = (f32[1024]{0:T(1024)S(1)}, f32[1024]{0:T(1024)}, u32[]{:S(2)}) copy-start(f32[1024]{0:T(1024)} %copy-done.28) | copy-start | bytes 12292
  2242.0 10.9 copy-start.1
  (15 other events, 64.0 us)
where the time goes:
time: 2270 us; the launch traced here: 2250 us
  waiting for transfers between devices  989 us (44%)
  local copies, waits for them, and re-layouts  704 us (31%)
  matrix products  405 us (18%)
  other arithmetic  130 us (6%)
  starting transfers between devices  23 us (1%)
    all_to_all x2, waiting for transfers between devices, local_program(): received = lax.all_to_all(send_buf, 'ep', 1, 1, tiled=True)  691 us
    gather x2, local copies, waits for them, and re-layouts, local_program(): per_copy = jnp.take(returned.reshape(buf_rows, width), buf_pos, axis=0)  300 us
    all_to_all x2, waiting for transfers between devices, local_program(): lax.all_to_all(expert_out.reshape(local_experts, group_size, capacity, wi...  298 us
    gather x2, local copies, waits for them, and re-layouts, local_program(): jnp.take(normed, source_row, axis=0, mode='fill', fill_value=0)  164 us
    gather x10, local copies, waits for them, and re-layouts, route(): picked = jnp.take_along_axis(logits, route_ids, axis=1)  134 us
    dot_general x2, matrix products, expert_ffn(): jnp.einsum('lrf,lfd->lrd', hidden, expert_down, preferred_element_type=jn...  94.5 us
    dot_general x2, matrix products, dense_branch(): jnp.einsum('bqgre,bkge->bgrqk', grouped, keys_rot, preferred_element_type...  74.9 us
    dot_general x2, matrix products, expert_ffn(): jnp.einsum('lrd,ldf->lrf', rows_in, expert_gate, preferred_element_type=j...  63.2 us
  transfers between devices with their start and end apart: 4, of which 4 were waited for; matrix products, arithmetic and copies ran while one was open for 37% of the time, Pallas kernels for 0%

commit v1 on v0

v1 whole, which is shorter than its diff:
```python
import functools

import jax
import jax.numpy as jnp
from jax import lax
from jax.experimental import pallas as pl
from jax.experimental.pallas import tpu as pltpu
from jax.sharding import PartitionSpec as P

EPS = 1e-6
ROPE_BASE = 10000.0


def rms_norm(values, scale):
    widened = values.astype(jnp.float32)
    mean_sq = jnp.mean(widened * widened, axis=-1, keepdims=True)
    return (widened * lax.rsqrt(mean_sq + EPS) * scale.astype(jnp.float32)).astype(jnp.bfloat16)


def rotary(values):
    seq_len = values.shape[-3]
    head_dim = values.shape[-1]
    half_dim = head_dim // 2
    freqs = ROPE_BASE ** (-jnp.arange(half_dim, dtype=jnp.float32) * 2.0 / head_dim)
    angles = jnp.arange(seq_len, dtype=jnp.float32)[:, None] * freqs[None, :]
    cosine = jnp.cos(angles)[:, None, :]
    sine = jnp.sin(angles)[:, None, :]
    first = values[..., :half_dim]
    second = values[..., half_dim:]
    return jnp.concatenate([first * cosine - second * sine, second * cosine + first * sine], axis=-1)


def dense_branch(resid, norm_attn, w_query, w_key, w_value, w_out, norm_ffn, w_gate, w_up, w_down):
    batch, seq_len = resid.shape[0], resid.shape[1]
    heads, head_dim = w_query.shape[1], w_query.shape[2]
    kv_heads = w_key.shape[1]
    normed = rms_norm(resid, norm_attn)
    queries = rotary(jnp.einsum('bsd,dhe->bshe', normed, w_query, preferred_element_type=jnp.float32)).astype(jnp.bfloat16)
    keys_rot = rotary(jnp.einsum('bsd,dhe->bshe', normed, w_key, preferred_element_type=jnp.float32)).astype(jnp.bfloat16)
    values_in = jnp.einsum('bsd,dhe->bshe', normed, w_value, preferred_element_type=jnp.float32).astype(jnp.bfloat16)
    grouped = queries.reshape(batch, seq_len, kv_heads, heads // kv_heads, head_dim)
    scores = jnp.einsum('bqgre,bkge->bgrqk', grouped, keys_rot, preferred_element_type=jnp.float32) * (head_dim ** -0.5)
    causal = jnp.arange(seq_len)[:, None] >= jnp.arange(seq_len)[None, :]
    probs = jax.nn.softmax(jnp.where(causal, scores, -1e30), axis=-1).astype(jnp.bfloat16)
    attended = jnp.einsum('bgrqk,bkge->bqgre', probs, values_in, preferred_element_type=jnp.float32).astype(jnp.bfloat16)
    attn_out = jnp.einsum('bshe,hed->bsd', attended.reshape(batch, seq_len, heads, head_dim), w_out, preferred_element_type=jnp.float32)
    after_attn = (resid.astype(jnp.float32) + attn_out).astype(jnp.bfloat16)
    normed_ffn = rms_norm(after_attn, norm_ffn)
    gate_act = jnp.einsum('bsd,df->bsf', normed_ffn, w_gate, preferred_element_type=jnp.float32)
    up_act = jnp.einsum('bsd,df->bsf', normed_ffn, w_up, preferred_element_type=jnp.float32)
    hidden = (jax.nn.silu(gate_act) * up_act).astype(jnp.bfloat16)
    down_act = jnp.einsum('bsf,fd->bsd', hidden, w_down, preferred_element_type=jnp.float32)
    return after_attn.astype(jnp.float32) + down_act


def route(normed, w_router, route_ids):
    logits = jnp.dot(normed, w_router, preferred_element_type=jnp.float32)
    experts = w_router.shape[1]
    picked = jnp.any(route_ids[:, :, None] == jnp.arange(experts, dtype=jnp.int32)[None, None, :], axis=1)
    top = jnp.max(jnp.where(picked, logits, -jnp.inf), axis=-1, keepdims=True)
    powers = jnp.where(picked, jnp.exp(jnp.where(picked, logits, top) - top), 0.0)
    return powers / jnp.sum(powers, axis=-1, keepdims=True)


def moe_kernel(row_tile, width, hidden, x_ref, gates_ref, base_ref, pack_ref, out_ref, total_ref):
    expert = pl.program_id(0)
    rows = x_ref.shape[0]

    @pl.when(expert == 0)
    def _():
        total_ref[...] = base_ref[...]

    lanes = lax.broadcasted_iota(jnp.int32, (row_tile, gates_ref.shape[1]), 1)

    def tile_step(tile, carry):
        part = pl.ds(pl.multiple_of(tile * row_tile, row_tile), row_tile)
        tokens = x_ref[part, :]
        weight = jnp.sum(jnp.where(lanes == expert, gates_ref[part, :], 0.0), axis=1, keepdims=True)
        gate_act = jnp.dot(tokens, pack_ref[0, :width, :], preferred_element_type=jnp.float32)
        up_act = jnp.dot(tokens, pack_ref[0, width:2 * width, :], preferred_element_type=jnp.float32)
        mixed = (jax.nn.silu(gate_act) * up_act).astype(jnp.bfloat16)
        for side in range(2):
            cols = pl.ds(side * (width // 2), width // 2)
            start = 2 * width + side * hidden
            down = jnp.dot(mixed, pack_ref[0, start:start + hidden, :], preferred_element_type=jnp.float32)
            down = down.astype(jnp.bfloat16).astype(jnp.float32)
            total_ref[part, cols] += jnp.where(weight > 0.0, weight * down, 0.0)
        return carry

    lax.fori_loop(0, rows // row_tile, tile_step, 0)

    @pl.when(expert == pl.num_programs(0) - 1)
    def _():
        out_ref[...] = total_ref[...].astype(out_ref.dtype)


def moe_all(tokens, gates, base, packed):
    rows, width = tokens.shape
    experts, pack_rows, hidden = packed.shape
    row_tile = 512
    once = pl.Buffered(buffer_count=1)
    return pl.pallas_call(
        functools.partial(moe_kernel, row_tile, width, hidden),
        out_shape=jax.ShapeDtypeStruct((rows, width), jnp.bfloat16),
        grid=(experts,),
        in_specs=[
            pl.BlockSpec((rows, width), lambda e: (0, 0), pipeline_mode=once),
            pl.BlockSpec((rows, gates.shape[1]), lambda e: (0, 0), pipeline_mode=once),
            pl.BlockSpec((rows, width), lambda e: (0, 0), pipeline_mode=once),
            pl.BlockSpec((1, pack_rows, hidden), lambda e: (e, 0, 0)),
        ],
        out_specs=pl.BlockSpec((rows, width), lambda e: (0, 0), pipeline_mode=once),
        scratch_shapes=[pltpu.VMEM((rows, width), jnp.float32)],
        compiler_params=pltpu.CompilerParams(dimension_semantics=("arbitrary",), vmem_limit_bytes=60 * 1024 * 1024),
        cost_estimate=pl.CostEstimate(flops=rows * experts * 6 * width * hidden, bytes_accessed=packed.size * 2, transcendentals=0),
    )(tokens, gates, base, packed)


def solution(mesh):
    tok_spec = P(None, ('dp', 'ep'), None, None)
    rep_one = P(None)
    rep_two = P(None, None)
    rep_three = P(None, None, None)
    expert_spec = P('ep', None, None)

    def local_program(resid_in, expert_idx, expert_slot, w_query, w_key, w_value, w_out, w_gate, w_up, w_down, w_router, norm_attn, norm_ffn, norm_moe, expert_gate, expert_up, expert_down):
        micro_count, seqs, seq_len, width = resid_in.shape
        choices = expert_idx.shape[-1]
        rows = micro_count * seqs * seq_len
        half = width // 2
        packed = jnp.concatenate([expert_gate, expert_up, expert_down[:, :, :half], expert_down[:, :, half:]], axis=1)
        packed = lax.all_gather(packed, 'ep', axis=0, tiled=True)
        resid = resid_in.reshape(micro_count * seqs, seq_len, width)
        tokens = rms_norm(resid.reshape(rows, width), norm_moe)
        gates = route(tokens, w_router, expert_idx.reshape(rows, choices))
        dense_out = dense_branch(resid, norm_attn, w_query, w_key, w_value, w_out, norm_ffn, w_gate, w_up, w_down)
        out = moe_all(tokens, gates, dense_out.reshape(rows, width), packed)
        return out.reshape(resid_in.shape)

    return jax.shard_map(local_program, mesh=mesh, in_specs=(tok_spec, tok_spec, tok_spec, rep_three, rep_three, rep_three, rep_three, rep_two, rep_two, rep_two, rep_two, rep_one, rep_one, rep_one, expert_spec, expert_spec, expert_spec), out_specs=tok_spec, check_vma=False)
```

time: 2270 us -> 555 us (0.24)
  waiting for transfers between devices: 989 us -> 63.2 us
  local copies, waits for them, and re-layouts: 704 us -> 5.52 us
  Pallas kernels: 0 us -> 246 us
  matrix products: 405 us -> 196 us
  other arithmetic: 130 us -> 23.5 us
  starting transfers between devices: 23 us -> 0.01 us
    all_to_all x4 -> x0, waiting for transfers between devices: 989 us -> none  [the longest x2 691 us: local_program(): received = lax.all_to_all(send_buf, 'ep', 1, 1, tiled=True)]
    gather x14 -> x0, local copies, waits for them, and re-layouts: 598 us -> none  [the longest x2 300 us: local_program(): per_copy = jnp.take(returned.reshape(buf_rows, width), buf_pos, axis=0)]
    pallas_call x0 -> x1, Pallas kernels: none -> 246 us  [moe_all(): pl.pallas_call(functools.partial(moe_kernel, row_tile, width, hidden), ou...]
    dot_general x6 -> x4, matrix products: 232 us -> 40.2 us  [the longest x1 29.1 us: dense_branch(): jnp.einsum('bsd,df->bsf', normed_ffn, w_up, preferred_element_type=jnp.fl...]
    all_gather x0 -> x1, waiting for transfers between devices: none -> 63.1 us  [local_program(): packed = lax.all_gather(packed, 'ep', axis=0, tiled=True)]
    scatter x2 -> x0, local copies, waits for them, and re-layouts: 61 us -> none  [local_program(): jnp.full((buf_rows,), tokens, jnp.int32).at[buf_pos.reshape(-1)]]
    reduce_sum x4 -> x1, other arithmetic: 59.2 us -> 1.32 us  [route(): return powers / jnp.sum(powers, axis=-1, keepdims=True)]
    sub x0 -> x1, matrix products: none -> 55.4 us  [dense_branch(): jax.nn.softmax(jnp.where(causal, scores, -1e+30), axis=-1)]
  transfers between devices with their start and end apart: 4 -> 1, of which waited for: 4 -> 1; matrix products, arithmetic and copies ran while one was open for 37% -> 40% of each run, Pallas kernels for 0% -> 0%
where the time goes in v1:
time: 555 us; the launch traced here: 548 us
  Pallas kernels  246 us (44%)
  matrix products  196 us (35%)
  waiting for transfers between devices  63.2 us (11%)
  other arithmetic  23.5 us (4%)
  between operations  14 us (3%)
    pallas_call x1, Pallas kernels, moe_all(): pl.pallas_call(functools.partial(moe_kernel, row_tile, width, hidden), ou...  246 us
    all_gather x1, waiting for transfers between devices, local_program(): packed = lax.all_gather(packed, 'ep', axis=0, tiled=True)  63.1 us
    sub x1, matrix products, dense_branch(): jax.nn.softmax(jnp.where(causal, scores, -1e+30), axis=-1)  55.4 us
    dot_general x1, matrix products, dense_branch(): jnp.einsum('bgrqk,bkge->bqgre', probs, values_in, preferred_element_type=...  44 us
    dot_general x1, matrix products, dense_branch(): jnp.einsum('bsd,df->bsf', normed_ffn, w_up, preferred_element_type=jnp.fl...  29.1 us
    dot_general x1, matrix products, dense_branch(): jnp.einsum('bsf,fd->bsd', hidden, w_down, preferred_element_type=jnp.floa...  24.3 us
    dot_general x1, matrix products, dense_branch(): jnp.einsum('bsd,df->bsf', normed_ffn, w_gate, preferred_element_type=jnp....  21.8 us
  transfers between devices with their start and end apart: 1, of which 1 were waited for; matrix products, arithmetic and copies ran while one was open for 40% of the time, Pallas kernels for 0%

profile of v1, /device:TPU:107, one launch (start us, length us, event | category | flops | bytes accessed | tf_op | source)
XLA Modules:
  0.0 548.1 jit_solution(3514207849537818691)
XLA Ops:
  6.6 1.4 fusion.62
  8.0 0.0 copy-start.16
  8.0 3.0 pad_maximum_fusion.1
  11.0 0.1 all-gather.2.cloned.1.call-update
  11.1 0.6 convert_element_type.74
  11.7 3.1 fusion.25
  14.8 0.3 fusion.48
  15.1 0.4 copy.37
  15.6 0.0 copy-start.11
  15.6 3.1 fusion.24.x_ref
  18.7 2.0 copy-done.4
  20.7 2.0 select_reduce_fusion
  22.7 1.3 copy.36
  24.0 1.3 iota_compare_fusion
  25.3 1.3 fusion.52
  26.7 3.1 fusion.20
  29.8 0.5 fusion.54
  30.3 2.5 fusion.40
  32.9 1.8 subtract_convert_fusion.1
  34.6 4.6 fusion.38
  39.2 3.4 subtract_convert_fusion
  42.7 4.0 fusion.42
  46.7 55.4 %fusion.63 = (f32[2,8,2,1024]{3,2,1,0:T(2,128)S(1)}, f32[2,8,2,1024,1024]{3,4,2,1,0:T(8,128)}) fusion(pred[1024,1024]{0,1:T(8,128)(4,1)} %iota_compare_fusion, bf16[2,1024,8,2,32]{1,4,3,2,0:T(8,128)(2,1)} %bitcast.122, bf16[2,1024,8,2,32]{1,4,3,2,0:T(8,128)(2,1)} %bitcast.121, bf16[2,1024,8,32]{1,3,2,0:T(8,128)(2,1)} %get-tuple-element.8, ...), kind=kOutput, calls=%fused_computation.75 | convolution fusion | flops 4441768960 | bytes 141688832 | tf_op jit(solution)/shard_map/sub | solution.py:44
  102.2 44.0 %fusion.37 = bf16[2,8,64,2,1024]{4,2,3,1,0:T(8,128)(2,1)} fusion(f32[2,8,2,1024,1024]{3,4,2,1,0:T(8,128)} %get-tuple-element.16, f32[2,8,2,1024]{3,2,1,0:T(2,128)S(1)} %get-tuple-element.15, bf16[2,1024,8,64]{1,3,2,0:T(8,128)(2,1)} %fusion.42), kind=kOutput, calls=%fused_computation.42 | convolution fusion | flops 4364173312 | bytes 140640256 | tf_op jit(solution)/shard_map/bgrqk,bkge->bqgre/dot_general | solution.py:45
  146.2 7.9 %fusion.11 = (f32[2,1024]{1,0:T(2,128)S(1)}, bf16[2,1024,1024]{2,1,0:T(8,128)(2,1)S(1)}) fusion(bf16[2,1024,16,64]{1,3,2,0:T(8,128)(2,1)} %bitcast.126, bf16[16,64,1024]{2,1,0:T(8,128)(2,1)S(1)} %copy-done, bf16[2,1,1024,1024]{3,2,1,0:T(8,128)(2,1)S(1)} %copy-done.3), kind=kOutput, calls=%fused_computation.16 | convolution fusion | flops 4307548160 | bytes 14688256 | tf_op jit(solution)/shard_map/bshe,hed->bsd/dot_general | solution.py:46
  154.2 2.0 fusion.51.gates_ref
  156.2 0.3 copy-done.22
  156.5 21.8 %fusion.17 = f32[2,1024,4096]{2,1,0:T(8,128)} fusion(bf16[1024,4096]{1,0:T(8,128)(2,1)S(1)} %copy-done.18, bf16[2,1024,1024]{2,1,0:T(8,128)(2,1)S(1)} %get-tuple-element.18, f32[1024]{0:T(1024)S(1)} %copy-done.14, f32[2,1024]{1,0:T(2,128)S(1)} %add_rsqrt_fusion), kind=kOutput, calls=%fused_computation.21 | convolution fusion | flops 17188257792 | bytes 46149632 | tf_op jit(solution)/shard_map/bsd,df->bsf/dot_general | solution.py:49
  178.3 29.1 %multiply_convert_fusion.6 = bf16[2,1024,4096]{2,1,0:T(8,128)(2,1)} fusion(f32[2,1024,4096]{2,1,0:T(8,128)} %fusion.17, bf16[1024,4096]{1,0:T(8,128)(2,1)} %param.24, bf16[2,1024,1024]{2,1,0:T(8,128)(2,1)} %copy-done.22, f32[1024]{0:T(1024)S(1)} %copy-done.14, f32[2,1024]{1,0:T(2,128)S(1)} %add_rsqrt_fusion), kind=kOutput, calls=%fused_computation.9.clone.clone.clone.clone.1 | convolution fusion | flops 17238589440 | bytes 62926848 | tf_op jit(solution)/shard_map/bsd,df->bsf/dot_general | solution.py:50
  207.3 24.3 %convert_add_fusion = f32[2,1024,1024]{2,1,0:T(8,128)} fusion(bf16[2,1024,1024]{2,1,0:T(8,128)(2,1)} %copy-done.22, bf16[4096,1024]{1,0:T(8,128)(2,1)} %param.25, bf16[2,1024,4096]{2,1,0:T(8,128)(2,1)} %multiply_convert_fusion.6), kind=kOutput, calls=%fused_computation.13 | convolution fusion | flops 17184063488 | bytes 37748736 | tf_op jit(solution)/shard_map/bsf,fd->bsd/dot_general | solution.py:52
  231.7 63.1 %all-gather.2.cloned.1.call-done.pack_ref = bf16[32,3072,512]{2,1,0:T(8,128)(2,1)} async-done(((bf16[1,3072,512]{2,1,0:T(8,128)(2,1)}), bf16[32,3072,512]{2,1,0:T(8,128)(2,1)}) %all-gather.2.cloned.1.call-update) | async-done | bytes 100663312 | tf_op jit(solution)/shard_map/all_gather | solution.py:132
  294.8 246.2 %shard_map.154 = bf16[2048,1024]{1,0:T(8,128)(2,1)} custom-call(bf16[2048,1024]{1,0:T(8,128)(2,1)} %copy-done.4, f32[2048,32]{1,0:T(8,128)} %fusion.51.gates_ref, f32[2048,1024]{1,0:T(8,128)} %bitcast.125, bf16[32,3072,512]{2,1,0:T(8,128)(2,1)} %all-gather.2.cloned.1.call-done.pack_ref), custom_call_target="tpu_custom_call" | custom-call | flops 206158430208 | bytes 100663296 | tf_op jit(solution)/shard_map/pallas_call | solution.py:102
  (50 shorter events, 0.2 us)
Async XLA Ops:
  6.5 139.6 %copy-start = (bf16[16,64,1024]{2,1,0:T(8,128)(2,1)S(1)}, bf16[16,64,1024]{2,1,0:T(8,128)(2,1)}, u32[]{:S(2)}) copy-start(bf16[16,64,1024]{2,1,0:T(8,128)(2,1)} %param.22) | copy-start | bytes 6291460
  6.6 288.3 %all-gather.2.cloned.1.call-start = ((), (), s32[]{:S(2)}) async-start(), calls=%async_computation | async-start | bytes 103809024 | tf_op jit(solution)/shard_map/all_gather | solution.py:132
  8.0 3.1 copy-start.15
  8.0 3.1 copy-start.16
  11.0 3.8 copy-start.17
  11.0 3.8 copy-start.12
  15.6 9.7 %copy-start.7 = (pred[2048,32]{1,0:T(8,128)(4,1)}, pred[2048,32]{1,0:T(8,128)(4,1)S(1)}, u32[]{:S(2)}) copy-start(pred[2048,32]{1,0:T(8,128)(4,1)S(1)} %copy.37) | copy-start | bytes 196612
  15.6 5.1 copy-start.11
  18.7 2.0 copy-start.4
  22.7 10.1 %copy-start.9 = (f32[2048]{0:T(1024)}, f32[2048]{0:T(1024)S(1)}, u32[]{:S(2)}) copy-start(f32[2048]{0:T(1024)S(1)} %get-tuple-element.13) | copy-start | bytes 24580
  24.0 8.8 %copy-start.5 = (f32[2048,32]{1,0:T(8,128)}, f32[2048,32]{1,0:T(8,128)S(1)}, u32[]{:S(2)}) copy-start(f32[2048,32]{1,0:T(8,128)S(1)} %copy.36) | copy-start | bytes 786436
  24.0 6.3 %copy-start.2 = (bf16[2,1,1024,1024]{3,2,1,0:T(8,128)(2,1)S(1)}, bf16[2,1,1024,1024]{3,2,1,0:T(8,128)(2,1)}, u32[]{:S(2)}) copy-start(bf16[2,1,1024,1024]{3,2,1,0:T(8,128)(2,1)} %param.17) | copy-start | bytes 12582916
  24.0 6.3 %copy-start.20 = (bf16[1024,8,64]{0,2,1:T(8,128)(2,1)S(1)}, bf16[1024,8,64]{0,2,1:T(8,128)(2,1)}, u32[]{:S(2)}) copy-start(bf16[1024,8,64]{0,2,1:T(8,128)(2,1)} %param.20) | copy-start | bytes 3145732
  32.9 1.8 copy-start.19
  39.2 3.4 copy-start.21
  102.1 44.0 %copy-start.3 = (bf16[2,1,1024,1024]{3,2,1,0:T(8,128)(2,1)S(1)}, bf16[2,1,1024,1024]{3,2,1,0:T(8,128)(2,1)}, u32[]{:S(2)}) copy-start(bf16[2,1,1024,1024]{3,2,1,0:T(8,128)(2,1)} %param.17) | copy-start | bytes 12582916
  146.2 8.0 %copy-start.6 = (f32[2048,32]{1,0:T(8,128)S(1)}, f32[2048,32]{1,0:T(8,128)}, u32[]{:S(2)}) copy-start(f32[2048,32]{1,0:T(8,128)} %copy-done.5) | copy-start | bytes 786436
  146.2 8.0 %copy-start.8 = (pred[2048,32]{1,0:T(8,128)(4,1)S(1)}, pred[2048,32]{1,0:T(8,128)(4,1)}, u32[]{:S(2)}) copy-start(pred[2048,32]{1,0:T(8,128)(4,1)} %copy-done.7) | copy-start | bytes 196612
  146.2 8.0 %copy-start.10 = (f32[2048]{0:T(1024)S(1)}, f32[2048]{0:T(1024)}, u32[]{:S(2)}) copy-start(f32[2048]{0:T(1024)} %copy-done.9) | copy-start | bytes 24580
  146.2 8.0 %copy-start.13 = (f32[2048]{0:T(1024)S(1)}, f32[2048]{0:T(1024)}, u32[]{:S(2)}) copy-start(f32[2048]{0:T(1024)} %fusion.52) | copy-start | bytes 24580
  146.2 10.2 %copy-start.14 = (f32[1024]{0:T(1024)S(1)}, f32[1024]{0:T(1024)}, u32[]{:S(2)}) copy-start(f32[1024]{0:T(1024)} %convert_element_type.74) | copy-start | bytes 12292
  146.2 10.2 %copy-start.18 = (bf16[1024,4096]{1,0:T(8,128)(2,1)S(1)}, bf16[1024,4096]{1,0:T(8,128)(2,1)}, u32[]{:S(2)}) copy-start(bf16[1024,4096]{1,0:T(8,128)(2,1)} %param.23) | copy-start | bytes 25165828
  154.1 2.3 copy-start.22
  294.8 246.2 %copy-start.1 = (bf16[16,64,1024]{2,1,0:T(8,128)(2,1)S(1)}, bf16[16,64,1024]{2,1,0:T(8,128)(2,1)}, u32[]{:S(2)}) copy-start(bf16[16,64,1024]{2,1,0:T(8,128)(2,1)} %param.22) | copy-start | bytes 6291460
Sparse Core Ops, SparseCore 0:
  11.2 283.6 all-gather.1

commit v2 on v0

v2 whole, which is shorter than its diff:
```python
import functools
import math

import jax
import jax.numpy as jnp
import numpy as np
from jax import lax
from jax.experimental import pallas as pl
from jax.experimental.pallas import tpu as pltpu
from jax.sharding import PartitionSpec as P

EPS = 1e-6
ROPE_BASE = 10000.0
LANES = 128
F32 = jnp.float32
BF16 = jnp.bfloat16

BLOCKS = ((0, 0), (1, 0), (3, 0), (0, 1), (0, 3), (1, 1), (1, 3), (3, 1), (3, 3), (2, 0), (0, 2), (2, 1), (1, 2), (2, 3), (3, 2), (2, 2))
SIDE = 4
STEPS = ((1, 0), (-1, 0), (0, 1), (0, -1))
GATE, UP, LOW, HIGH = 0, 1, 2, 3


def block_of(dx, dy):
    return BLOCKS.index((dx % SIDE, dy % SIDE))


def send_plan():
    plan = [[], [], [], [], []]
    used = [0, 0, 0, 0]

    def send(service, link, pieces, dx, dy):
        sx, sy = STEPS[link]
        for piece in pieces:
            plan[service].append((link, used[link], piece, block_of(dx, dy), block_of(dx + sx, dy + sy)))
            used[link] += 1

    send(0, 0, (GATE, LOW, UP, HIGH), 0, 0)
    send(0, 1, (LOW, GATE, HIGH, UP), 0, 0)
    send(0, 2, (UP, HIGH, GATE, LOW), 0, 0)
    send(0, 3, (HIGH, UP, LOW, GATE), 0, 0)

    low_first, gate_first, up_first, high_first = (LOW, GATE), (GATE, LOW), (UP, HIGH), (HIGH, UP)
    for link, piece, near in ((0, GATE, (1, 0)), (1, LOW, (3, 0)), (2, UP, (0, 1)), (3, HIGH, (0, 3))):
        send(1, link, (piece,), *near)
    for near in (1, 3):
        for link, pieces in enumerate((up_first, high_first)):
            send(1, link, pieces, 0, near)
        for link, pieces in enumerate((gate_first, low_first)):
            send(1, 2 + link, pieces, near, 0)

    for link, piece, near in ((0, HIGH, (1, 0)), (1, UP, (3, 0)), (2, LOW, (0, 1)), (3, GATE, (0, 3))):
        send(2, link, (piece,), *near)
    for link, pieces in enumerate((up_first, high_first)):
        send(2, link, pieces, 0, 2)
    for link, pieces in enumerate((gate_first, low_first)):
        send(2, 2 + link, pieces, 2, 0)

    for near in (1, 3):
        for link, piece, far in ((0, UP, (1, near)), (1, HIGH, (3, near)), (2, GATE, (near, 1)), (3, LOW, (near, 3))):
            send(3, link, (piece,), *far)

    for link, piece, near in ((0, HIGH, (1, 2)), (1, UP, (3, 2)), (2, LOW, (2, 1)), (3, GATE, (2, 3))):
        send(4, link, (piece,), *near)
    return plan


def wait_plan():
    both, first, second = (GATE, LOW, UP, HIGH), (GATE, LOW), (UP, HIGH)
    waits = [
        [],
        [((1, 0), first), ((3, 0), first), ((0, 1), second), ((0, 3), second)],
        [((1, 0), second), ((3, 0), second), ((0, 1), first), ((0, 3), first), ((2, 0), first), ((0, 2), second)],
        [((1, 1), both), ((1, 3), both), ((3, 1), both), ((3, 3), both)],
        [((2, 0), second), ((0, 2), first), ((2, 1), first), ((2, 3), first), ((1, 2), second), ((3, 2), second)],
        [((1, 2), first), ((3, 2), first), ((2, 1), second), ((2, 3), second), ((2, 2), both)],
    ]
    done = [
        [(0, 0)],
        [],
        [(1, 0), (3, 0), (0, 1), (0, 3)],
        [(1, 1), (1, 3), (3, 1), (3, 3)],
        [(2, 0), (0, 2)],
        [(2, 1), (1, 2), (2, 3), (3, 2), (2, 2)],
    ]
    return waits, done


def matmul(left, right):
    return jnp.dot(left, right, preferred_element_type=F32)


def matmul_t(left, right):
    return lax.dot_general(left, right, (((1,), (1,)), ((), ())), preferred_element_type=F32)


def norm_scale_of(values):
    return lax.rsqrt(jnp.mean(values * values, axis=-1, keepdims=True) + EPS)


def fused_kernel(
    dims,
    x_hbm, ids_hbm, router_hbm, norms_hbm, rope_hbm, wq_hbm, wk_hbm, wv_hbm, wo_hbm, fg_hbm, fu_hbm, fd_hbm, eg_hbm, eu_hbm, ed_hbm,
    out_hbm, gg_hbm, gu_hbm, gd_hbm,
    xs, acc, gates, qs, ks, vs, os, s_outer, s_inner, p_outer, p_inner, tops, sums, ids, router, norms, rope, wqkv, wo, wg, wu, wd,
    load_sem, w_sem, out_sem, ici_send, ici_recv, d2d_send, d2d_recv,
):
    rows, width, seq, hidden, heads, kv_heads, head = dims
    micro = rows // seq
    half = hidden // 2
    experts = 2 * len(BLOCKS)
    ffn_steps = fg_hbm.shape[1] // hidden
    steps = ffn_steps + experts
    me = lax.axis_index('ep')
    core = lax.rem(me, 2)
    col = lax.rem(me // 2, SIDE)
    row = me // (2 * SIDE)

    def device(dx, dy, flip):
        cx = lax.rem(col + dx + SIDE, SIDE)
        cy = lax.rem(row + dy + SIDE, SIDE)
        return {'ep': (cy * SIDE + cx) * 2 + lax.rem(core + flip, 2)}

    def piece_ref(block, piece):
        if block == 0:
            return (eg_hbm.at[0], eu_hbm.at[0], ed_hbm.at[0, pl.ds(0, half)], ed_hbm.at[0, pl.ds(half, half)])[piece]
        return slot_ref(2 * block, piece)

    def slot_ref(slot, piece):
        return (gg_hbm.at[slot], gu_hbm.at[slot], gd_hbm.at[slot, pl.ds(0, half)], gd_hbm.at[slot, pl.ds(half, half)])[piece]

    def ici_copy(link, place, piece, source, target):
        return pltpu.make_async_remote_copy(
            src_ref=piece_ref(source, piece), dst_ref=slot_ref(2 * target, piece),
            send_sem=ici_send.at[link, place], recv_sem=ici_recv.at[target, piece],
            device_id=device(*STEPS[link], 0), device_id_type=pl.DeviceIdType.MESH)

    def d2d_copies(block, own):
        sources = (eg_hbm.at[0], eu_hbm.at[0], ed_hbm.at[0]) if own else (gg_hbm.at[2 * block], gu_hbm.at[2 * block], gd_hbm.at[2 * block])
        targets = (gg_hbm.at[2 * block + 1], gu_hbm.at[2 * block + 1], gd_hbm.at[2 * block + 1])
        return [pltpu.make_async_remote_copy(
            src_ref=sources[k], dst_ref=targets[k], send_sem=d2d_send.at[block, k], recv_sem=d2d_recv.at[block, k],
            device_id=device(0, 0, 1), device_id_type=pl.DeviceIdType.MESH) for k in range(3)]

    plan = send_plan()
    waits, done = wait_plan()
    arrival = {(target, piece): (link, place, piece, source, target) for stage in plan for link, place, piece, source, target in stage}

    def service(point):
        for (dx, dy), pieces in waits[point]:
            for piece in pieces:
                ici_copy(*arrival[(block_of(dx, dy), piece)]).wait_recv()
        if point < len(plan):
            for entry in plan[point]:
                ici_copy(*entry).start()
        for dx, dy in done[point]:
            for copy in d2d_copies(block_of(dx, dy), (dx, dy) == (0, 0)):
                copy.start()

    loads = [
        (x_hbm, xs.at[1]), (norms_hbm, norms), (router_hbm, router), (ids_hbm, ids), (rope_hbm, rope),
        (wq_hbm.at[pl.ds(0, 512)], wqkv.at[0]), (wq_hbm.at[pl.ds(512, 512)], wqkv.at[1]), (wk_hbm, wqkv.at[2]), (wv_hbm, wqkv.at[3]),
        (wo_hbm.at[pl.ds(0, 512)], wo.at[0]), (wo_hbm.at[pl.ds(512, 512)], wo.at[1]),
    ]
    loads = [pltpu.make_async_copy(source, target, load_sem.at[k]) for k, (source, target) in enumerate(loads)]
    for copy in loads:
        copy.start()

    barrier = pltpu.get_barrier_semaphore()
    for peer in [device(*step, 0) for step in STEPS] + [device(0, 0, 1)]:
        pl.semaphore_signal(barrier, inc=1, device_id=peer, device_id_type=pl.DeviceIdType.MESH)
    pl.semaphore_wait(barrier, len(STEPS) + 1)
    service(0)

    def expert_copies(slot, sources):
        return [pltpu.make_async_copy(source, buffer.at[slot], w_sem.at[slot, k]) for k, (source, buffer) in enumerate(zip(sources, (wg, wu, wd)))]

    def prefetch(step, slot):
        @pl.when(step < ffn_steps)
        def _():
            cut = pl.ds(pl.multiple_of(step * hidden, hidden), hidden)
            for copy in expert_copies(slot, (fg_hbm.at[:, cut], fu_hbm.at[:, cut], fd_hbm.at[cut])):
                copy.start()

        @pl.when(step == ffn_steps)
        def _():
            for copy in expert_copies(slot, (eg_hbm.at[0], eu_hbm.at[0], ed_hbm.at[0])):
                copy.start()

        @pl.when((step > ffn_steps) & (step < steps))
        def _():
            rank = step - ffn_steps

            @pl.when(lax.rem(rank, 2) == 1)
            def _():
                for copy in d2d_copies(rank // 2, False):
                    copy.wait_recv()

            for copy in expert_copies(slot, (gg_hbm.at[rank], gu_hbm.at[rank], gd_hbm.at[rank])):
                copy.start()

    prefetch(0, 0)

    for copy in loads[:4]:
        copy.wait()
    ranks = lax.broadcasted_iota(jnp.int32, (experts, 1), 0)
    owner = jnp.zeros((experts, 1), jnp.int32)
    for block, (dx, dy) in enumerate(BLOCKS):
        chip = lax.rem(row - dy + SIDE, SIDE) * SIDE + lax.rem(col - dx + SIDE, SIDE)
        owner = jnp.where(ranks // 2 == block, chip, owner)
    owner = owner * 2 + lax.rem(core + lax.rem(ranks, 2), 2)
    ordered = (lax.broadcasted_iota(jnp.int32, (experts, experts), 1) == owner).astype(F32).astype(BF16)
    ordered = matmul(ordered, router[...]).astype(BF16)
    tile = 512

    def prologue(index, carry):
        part = pl.ds(pl.multiple_of(index * tile, tile), tile)
        values = xs[1, part, :].astype(F32)
        unit = values * norm_scale_of(values)
        tokens = (unit * norms[2:3, :]).astype(BF16)
        xs[0, part, :] = (unit * norms[0:1, :]).astype(BF16)
        xs[1, part, :] = tokens
        acc[part, :] = values
        logits = matmul_t(ordered, tokens)
        per_seq = seq // tile
        picks = ids[index // per_seq, :, pl.ds(pl.multiple_of(lax.rem(index, per_seq) * tile, tile), tile)]
        picked = picks[0:1, :] == owner
        for choice in range(1, picks.shape[0]):
            picked = picked | (picks[choice:choice + 1, :] == owner)
        top = jnp.max(jnp.where(picked, logits, -jnp.inf), axis=0, keepdims=True)
        powers = jnp.where(picked, jnp.exp(jnp.where(picked, logits, top) - top), 0.0)
        share = powers / jnp.sum(powers, axis=0, keepdims=True)
        share = jnp.concatenate([share, jnp.zeros((LANES - experts, tile), F32)], axis=0)
        gates[part, :] = share.T
        return carry

    lax.fori_loop(0, rows // tile, prologue, 0)
    for copy in loads[4:]:
        copy.wait()

    def sequence(micro_index, carry):
        base = pl.multiple_of(micro_index * seq, seq)

        @pl.when(micro_index == 1)
        def _():
            service(1)

        lane = lax.broadcasted_iota(jnp.int32, (seq, LANES), 1)
        first = lax.rem(lane, head) < head // 2
        low = lane < head
        cosine, sine = rope[0], rope[1]
        tokens = xs[0, pl.ds(base, seq), :]

        def rotated(values):
            swapped = jnp.where(first, pltpu.roll(values, LANES - head // 2, 1), pltpu.roll(values, head // 2, 1))
            return values * cosine + swapped * sine

        def doubled(values, target, pair):
            turned = pltpu.roll(values, head, 1)
            place = 2 * pair * LANES
            target[:, place:place + LANES] = jnp.where(low, values, turned).astype(BF16)
            target[:, place + LANES:place + 2 * LANES] = jnp.where(low, turned, values).astype(BF16)

        for block in range(4):
            flat = matmul_t(tokens, wqkv[block])
            for piece in range(512 // LANES):
                values = flat[:, piece * LANES:(piece + 1) * LANES]
                if block < 2:
                    place = block * 512 + piece * LANES
                    qs[:, place:place + LANES] = (rotated(values) * head ** -0.5).astype(BF16)
                elif block == 2:
                    doubled(rotated(values), ks, piece)
                else:
                    doubled(values, vs, piece)

        chunk = 256
        chunk_low = lax.broadcasted_iota(jnp.int32, (chunk, LANES), 1) < head
        inside = lax.rem(lax.broadcasted_iota(jnp.int32, (2 * chunk, chunk), 0), chunk) >= lax.broadcasted_iota(jnp.int32, (2 * chunk, chunk), 1)

        def columns(index):
            return pl.ds(pl.multiple_of(index * LANES, LANES), LANES)

        def score(index, parts, target):
            cols, place = columns(index), 0
            for part in parts:
                span = (part + 1) * chunk
                q_part = qs[part * chunk:span, cols]
                none = jnp.zeros_like(q_part)
                pair = jnp.concatenate([jnp.where(chunk_low, q_part, none), jnp.where(chunk_low, none, q_part)], axis=0)
                scores = matmul_t(pair, ks[:span, cols])
                edge = jnp.where(inside, scores[:, part * chunk:], -1e30)
                scores = edge if part == 0 else jnp.concatenate([scores[:, :part * chunk], edge], axis=1)
                target[:, place:place + span] = scores
                tops[part] = jnp.broadcast_to(jnp.max(scores, axis=1, keepdims=True), tops.shape[1:])
                place += span

        def soften(parts, origin, target):
            place = 0
            for part in parts:
                top = tops[part]
                total = jnp.zeros_like(top)
                for _ in range((part + 1) * chunk // LANES):
                    powers = jnp.exp(origin[:, place:place + LANES] - top)
                    total = total + powers
                    target[:, place:place + LANES] = powers.astype(BF16)
                    place += LANES
                sums[part] = jnp.broadcast_to(jnp.sum(total, axis=1, keepdims=True), sums.shape[1:])

        def mix(index, parts, origin):
            cols, place = columns(index), 0
            for part in parts:
                span = (part + 1) * chunk
                mixed = matmul(origin[:, place:place + span], vs[:span, cols]) / sums[part]
                os[part * chunk:span, cols] = jnp.where(chunk_low, mixed[:chunk], mixed[chunk:]).astype(BF16)
                place += span

        outer_parts, inner_parts = (0, 3), (1, 2)
        score(0, outer_parts, s_outer)

        def group(index, inner):
            score(index, inner_parts, s_inner)
            soften(outer_parts, s_outer, p_outer)
            mix(lax.rem(index + kv_heads - 1, kv_heads), inner_parts, p_inner)
            score(lax.rem(index + 1, kv_heads), outer_parts, s_outer)
            soften(inner_parts, s_inner, p_inner)
            mix(index, outer_parts, p_outer)
            return inner

        lax.fori_loop(0, kv_heads, group, 0)
        mix(kv_heads - 1, inner_parts, p_inner)

        def project(index, inner):
            local = pl.ds(pl.multiple_of(index * tile, tile), tile)
            part = pl.ds(pl.multiple_of(base + index * tile, tile), tile)
            added = matmul(os[local, :tile], wo[0]) + matmul(os[local, tile:], wo[1])
            after = (acc[part, :] + added).astype(BF16).astype(F32)
            acc[part, :] = after
            xs[0, part, :] = (after * norm_scale_of(after) * norms[1:2, :]).astype(BF16)
            return inner

        lax.fori_loop(0, seq // tile, project, 0)
        return carry

    lax.fori_loop(0, micro, sequence, 0)

    big = 1024
    lanes = lax.broadcasted_iota(jnp.int32, (big, LANES), 1)
    moments = {ffn_steps // 2: 2, ffn_steps + 4: 3, ffn_steps + 11: 4, ffn_steps + 18: 5}

    def ffn_step(step, carry):
        slot = lax.rem(step, 2)
        for copy in expert_copies(slot, (gg_hbm.at[0], gu_hbm.at[0], gd_hbm.at[0])):
            copy.wait()
        for moment, point in moments.items():
            @pl.when(step == moment)
            def _():
                service(point)

        prefetch(step + 1, 1 - slot)
        dense = step < ffn_steps
        source = (step + steps - ffn_steps) // steps
        gate_w, up_w, down_w = wg.at[slot], wu.at[slot], wd.at[slot]

        def rows_step(index, inner):
            part = pl.ds(pl.multiple_of(index * big, big), big)
            tokens = xs[source, part, :]
            weight = jnp.sum(jnp.where(lanes == step - ffn_steps, gates[part, :], 0.0), axis=1, keepdims=True)
            weight = jnp.where(dense, 1.0, weight)
            gate_act = matmul(tokens, gate_w[...])
            up_act = matmul(tokens, up_w[...])
            mixed = (jax.nn.silu(gate_act) * up_act).astype(BF16)
            down = matmul(mixed, down_w[...])
            down = jnp.where(dense, down, down.astype(BF16).astype(F32))
            acc[part, :] += jnp.where(weight > 0.0, weight * down, 0.0)
            return inner

        lax.fori_loop(0, rows // big, rows_step, 0)
        return carry

    lax.fori_loop(0, steps, ffn_step, 0)

    def store(index):
        part = pl.ds(index * tile, tile)
        return pltpu.make_async_copy(xs.at[0, part], out_hbm.at[part], out_sem.at[index])

    for index in range(rows // tile):
        xs[0, index * tile:(index + 1) * tile, :] = acc[index * tile:(index + 1) * tile, :].astype(BF16)
        store(index).start()
    for stage in plan:
        for entry in stage:
            ici_copy(*entry).wait_send()
    for block in range(len(BLOCKS)):
        for copy in d2d_copies(block, block == 0):
            copy.wait_send()
    for index in range(rows // tile):
        store(index).wait()


def rope_tables(seq, head):
    half = head // 2
    freqs = np.float32(ROPE_BASE) ** (-np.arange(half, dtype=np.float32) * np.float32(2.0) / np.float32(head))
    angles = np.arange(seq, dtype=np.float32)[:, None] * freqs.astype(np.float32)[None, :]
    cosine = np.cos(angles.astype(np.float64)).astype(np.float32)
    sine = np.sin(angles.astype(np.float64)).astype(np.float32)
    times = LANES // head
    return np.stack([np.tile(np.concatenate([cosine, cosine], 1), (1, times)), np.tile(np.concatenate([-sine, sine], 1), (1, times))])


def solution(mesh):
    tok_spec = P(None, ('dp', 'ep'), None, None)
    rep_one = P(None)
    rep_two = P(None, None)
    rep_three = P(None, None, None)
    expert_spec = P('ep', None, None)
    assert mesh.shape['ep'] == 2 * SIDE * SIDE

    def local_program(resid_in, expert_idx, expert_slot, w_query, w_key, w_value, w_out, w_gate, w_up, w_down, w_router, norm_attn, norm_ffn, norm_moe, expert_gate, expert_up, expert_down):
        micro, seqs, seq, width = resid_in.shape
        choices = expert_idx.shape[-1]
        heads, head = w_query.shape[1:]
        kv_heads = w_key.shape[1]
        hidden = expert_gate.shape[2]
        experts = 2 * len(BLOCKS)
        rows = micro * seqs * seq
        ids = expert_idx.transpose(0, 1, 3, 2).reshape(micro * seqs, choices, seq)
        norms = jnp.stack([norm_attn, norm_ffn, norm_moe]).astype(F32)
        rope = jnp.asarray(rope_tables(seq, head))
        anywhere = pl.BlockSpec(memory_space=pl.ANY)
        operands = (
            resid_in.reshape(rows, width), ids, w_router.T, norms, rope,
            w_query.transpose(1, 2, 0).reshape(heads * head, width), w_key.transpose(1, 2, 0).reshape(kv_heads * head, width),
            w_value.transpose(1, 2, 0).reshape(kv_heads * head, width), w_out.reshape(heads * head, width),
            w_gate, w_up, w_down, expert_gate, expert_up, expert_down)
        flops = rows * width * 2 * (3 * hidden * experts + 3 * w_gate.shape[1] + 3 * heads * head)
        out = pl.pallas_call(
            functools.partial(fused_kernel, (rows, width, seq, hidden, heads, kv_heads, head)),
            out_shape=(
                jax.ShapeDtypeStruct((rows, width), BF16),
                jax.ShapeDtypeStruct((experts, width, hidden), BF16),
                jax.ShapeDtypeStruct((experts, width, hidden), BF16),
                jax.ShapeDtypeStruct((experts, hidden, width), BF16)),
            in_specs=[anywhere] * len(operands),
            out_specs=[anywhere] * 4,
            scratch_shapes=[
                pltpu.VMEM((2, rows, width), BF16),
                pltpu.VMEM((rows, width), F32),
                pltpu.VMEM((rows, LANES), F32),
                pltpu.VMEM((seq, heads * head), BF16),
                pltpu.VMEM((seq, kv_heads * LANES), BF16),
                pltpu.VMEM((seq, kv_heads * LANES), BF16),
                pltpu.VMEM((seq, heads * head), BF16),
                *[pltpu.VMEM((512, 1280), kind) for kind in (F32, F32, BF16, BF16)],
                *[pltpu.VMEM((4, 512, LANES), F32) for _ in range(2)],
                pltpu.VMEM((micro * seqs, choices, seq), jnp.int32),
                pltpu.VMEM((experts, width), BF16),
                pltpu.VMEM((3, width), F32),
                pltpu.VMEM((2, seq, LANES), F32),
                pltpu.VMEM((4, 512, width), BF16),
                pltpu.VMEM((2, 512, width), BF16),
                *[pltpu.VMEM((2,) + shape, BF16) for shape in ((width, hidden), (width, hidden), (hidden, width))],
                *[pltpu.SemaphoreType.DMA(shape) for shape in ((11,), (2, 3), (4,), (4, 15), (16, 4), (16, 3), (16, 3))],
            ],
            compiler_params=pltpu.CompilerParams(collective_id=0, has_side_effects=True, vmem_limit_bytes=62 * 1024 * 1024),
            cost_estimate=pl.CostEstimate(flops=flops, bytes_accessed=experts * 6 * width * hidden, transcendentals=0),
        )(*operands)[0]
        return out.reshape(resid_in.shape)

    return jax.shard_map(local_program, mesh=mesh, in_specs=(tok_spec, tok_spec, tok_spec, rep_three, rep_three, rep_three, rep_three, rep_two, rep_two, rep_two, rep_two, rep_one, rep_one, rep_one, expert_spec, expert_spec, expert_spec), out_specs=tok_spec, check_vma=False)
```

time: 2270 us -> 384 us (0.17)
  waiting for transfers between devices: 989 us -> 0 us
  local copies, waits for them, and re-layouts: 704 us -> 6.7 us
  matrix products: 405 us -> 0 us
  Pallas kernels: 0 us -> 372 us
  other arithmetic: 130 us -> 0.62 us
  starting transfers between devices: 23 us -> 0 us
    all_to_all x4 -> x0, waiting for transfers between devices: 989 us -> none  [the longest x2 691 us: local_program(): received = lax.all_to_all(send_buf, 'ep', 1, 1, tiled=True)]
    gather x14 -> x0, local copies, waits for them, and re-layouts: 598 us -> none  [the longest x2 300 us: local_program(): per_copy = jnp.take(returned.reshape(buf_rows, width), buf_pos, axis=0)]
    dot_general x16 -> x0, matrix products: 392 us -> none  [the longest x2 94.5 us: expert_ffn(): jnp.einsum('lrf,lfd->lrd', hidden, expert_down, preferred_element_type=jn...]
    pallas_call x0 -> x1, Pallas kernels: none -> 372 us  [local_program(): pl.pallas_call(functools.partial(fused_kernel, (rows, width, seq, hidden,...]
    reduce_sum x8 -> x0, other arithmetic: 66.4 us -> none  [the longest x2 37.3 us: local_program(): moe_out = jnp.sum(gates[:, :, None] * per_copy.astype(jnp.float32), axis=1)]
    scatter x2 -> x0, local copies, waits for them, and re-layouts: 61 us -> none  [local_program(): jnp.full((buf_rows,), tokens, jnp.int32).at[buf_pos.reshape(-1)]]
    select_n x4 -> x0, other arithmetic: 45.4 us -> none  [the longest x2 45.4 us: local_program(): jnp.take(normed, source_row, axis=0, mode='fill', fill_value=0)]
    all_to_all x4 -> x0, starting transfers between devices: 23 us -> none  [the longest x2 12.8 us: local_program(): received = lax.all_to_all(send_buf, 'ep', 1, 1, tiled=True)]
  transfers between devices with their start and end apart: 4 -> 0, of which waited for: 4 -> 0; matrix products, arithmetic and copies ran while one was open for 37% -> 0% of each run, Pallas kernels for 0% -> 0%
where the time goes in v2:
time: 384 us; the launch traced here: 379 us
  Pallas kernels  372 us (97%)
  local copies, waits for them, and re-layouts  6.7 us (2%)
    pallas_call x1, Pallas kernels, local_program(): pl.pallas_call(functools.partial(fused_kernel, (rows, width, seq, hidden,...  372 us

profile of v2, /device:TPU:107, one launch (start us, length us, event | category | flops | bytes accessed | tf_op | source)
XLA Modules:
  0.0 379.4 jit_solution(6637312492525764880)
XLA Ops:
  0.0 0.7 stack.12
  0.7 0.7 stack.13
  1.4 0.7 stack.14
  2.1 0.6 maximum_convert_fusion.norms_hbm
  2.7 372.0 %shard_map.163 = (bf16[2048,1024]{1,0:T(8,128)(2,1)}, bf16[32,1024,512]{2,1,0:T(8,128)(2,1)}, bf16[32,1024,512]{2,1,0:T(8,128)(2,1)}, bf16[32,512,1024]{2,1,0:T(8,128)(2,1)}) custom-call(bf16[2048,1024]{1,0:T(8,128)(2,1)} %bitcast.21, s32[2,8,1024]{2,1,0:T(8,128)} %bitcast.26, bf16[32,1024]{1,0:T(8,128)(2,1)} %bitcast.27, ...), custom_call_target="tpu_custom_call" | custom-call | flops 270582939648 | bytes 100663296 | tf_op jit(solution)/shard_map/pallas_call | solution.py:435
  374.7 4.6 %copy.21 = bf16[2,1,1024,1024]{3,2,1,0:T(8,128)(2,1)} copy(bf16[2,1,1024,1024]{3,2,1,0:T(8,128)(2,1)} %bitcast.20) | data formatting | bytes 8388608

commit v3 on v2

--- a/solution.py
+++ b/solution.py
@@ -15,10 +15,20 @@
 F32 = jnp.float32
 BF16 = jnp.bfloat16
 
-BLOCKS = ((0, 0), (1, 0), (3, 0), (0, 1), (0, 3), (1, 1), (1, 3), (3, 1), (3, 3), (2, 0), (0, 2), (2, 1), (1, 2), (2, 3), (3, 2), (2, 2))
+UNIT = 8
+TILE = 256
+STATIC = 16
+
 SIDE = 4
+NEAR = (1, 3)
+BLOCKS = (
+    (0, 0), *[(a, 0) for a in NEAR], *[(0, a) for a in NEAR], *[(a, b) for a in NEAR for b in NEAR],
+    *[place for a in (0, *NEAR) for place in ((2, a), (a, 2))], (2, 2))
 STEPS = ((1, 0), (-1, 0), (0, 1), (0, -1))
-GATE, UP, LOW, HIGH = 0, 1, 2, 3
+GATE, UP, LOW, HIGH, LOW_A, LOW_B, HIGH_A, HIGH_B = range(8)
+X_FIRST, Y_FIRST = (GATE, LOW), (UP, HIGH)
+ALL = (*X_FIRST, *Y_FIRST)
+LAST = ((1, 2), (3, 2), (2, 1), (2, 3))
 
 
 def block_of(dx, dy):
@@ -26,8 +36,8 @@
 
 
 def send_plan():
-    plan = [[], [], [], [], []]
-    used = [0, 0, 0, 0]
+    plan = [[] for _ in range(5)]
+    used = [0] * len(STEPS)
 
     def send(service, link, pieces, dx, dy):
         sx, sy = STEPS[link]
@@ -35,55 +45,51 @@
             plan[service].append((link, used[link], piece, block_of(dx, dy), block_of(dx + sx, dy + sy)))
             used[link] += 1
 
-    send(0, 0, (GATE, LOW, UP, HIGH), 0, 0)
-    send(0, 1, (LOW, GATE, HIGH, UP), 0, 0)
-    send(0, 2, (UP, HIGH, GATE, LOW), 0, 0)
-    send(0, 3, (HIGH, UP, LOW, GATE), 0, 0)
-
-    low_first, gate_first, up_first, high_first = (LOW, GATE), (GATE, LOW), (UP, HIGH), (HIGH, UP)
-    for link, piece, near in ((0, GATE, (1, 0)), (1, LOW, (3, 0)), (2, UP, (0, 1)), (3, HIGH, (0, 3))):
-        send(1, link, (piece,), *near)
-    for near in (1, 3):
-        for link, pieces in enumerate((up_first, high_first)):
-            send(1, link, pieces, 0, near)
-        for link, pieces in enumerate((gate_first, low_first)):
-            send(1, 2 + link, pieces, near, 0)
-
-    for link, piece, near in ((0, HIGH, (1, 0)), (1, UP, (3, 0)), (2, LOW, (0, 1)), (3, GATE, (0, 3))):
-        send(2, link, (piece,), *near)
-    for link, pieces in enumerate((up_first, high_first)):
-        send(2, link, pieces, 0, 2)
-    for link, pieces in enumerate((gate_first, low_first)):
-        send(2, 2 + link, pieces, 2, 0)
-
-    for near in (1, 3):
-        for link, piece, far in ((0, UP, (1, near)), (1, HIGH, (3, near)), (2, GATE, (near, 1)), (3, LOW, (near, 3))):
-            send(3, link, (piece,), *far)
-
-    for link, piece, near in ((0, HIGH, (1, 2)), (1, UP, (3, 2)), (2, LOW, (2, 1)), (3, GATE, (2, 3))):
-        send(4, link, (piece,), *near)
+    def spread(service, dx, dy):
+        pieces, start = (X_FIRST, 2) if dy == 0 else (Y_FIRST, 0)
+        send(service, start, pieces, dx, dy)
+        send(service, start + 1, pieces[::-1], dx, dy)
+
+    def relay(service, pieces, blocks):
+        for link, (piece, block) in enumerate(zip(pieces, blocks)):
+            send(service, link, (piece,), *block)
+
+    for link, order in enumerate((X_FIRST, X_FIRST[::-1], Y_FIRST, Y_FIRST[::-1])):
+        send(0, link, order, 0, 0)
+    for link, order in enumerate((Y_FIRST, Y_FIRST[::-1], X_FIRST, X_FIRST[::-1])):
+        send(0, link, order, 0, 0)
+
+    relay(1, (GATE, LOW, UP, HIGH), BLOCKS[1:5])
+    for a in NEAR:
+        spread(1, 0, a)
+        spread(1, a, 0)
+    relay(2, (HIGH, UP, LOW, GATE), BLOCKS[1:5])
+    spread(2, 0, 2)
+    spread(2, 2, 0)
+    for a in NEAR:
+        relay(3, (UP, HIGH, GATE, LOW), ((1, a), (3, a), (a, 1), (a, 3)))
+    relay(4, (HIGH_A, UP, LOW_A, GATE), LAST)
+    for link, piece in ((1, HIGH_B), (3, LOW_B)):
+        send(4, link, (piece,), *LAST[link])
     return plan
 
 
 def wait_plan():
-    both, first, second = (GATE, LOW, UP, HIGH), (GATE, LOW), (UP, HIGH)
-    waits = [
+    rows, cols = [(a, 0) for a in NEAR], [(0, a) for a in NEAR]
+    far_rows, far_cols = [(2, a) for a in NEAR], [(a, 2) for a in NEAR]
+
+    def need(first, second):
+        return [(block, X_FIRST) for block in first] + [(block, Y_FIRST) for block in second]
+
+    return [
         [],
-        [((1, 0), first), ((3, 0), first), ((0, 1), second), ((0, 3), second)],
-        [((1, 0), second), ((3, 0), second), ((0, 1), first), ((0, 3), first), ((2, 0), first), ((0, 2), second)],
-        [((1, 1), both), ((1, 3), both), ((3, 1), both), ((3, 3), both)],
-        [((2, 0), second), ((0, 2), first), ((2, 1), first), ((2, 3), first), ((1, 2), second), ((3, 2), second)],
-        [((1, 2), first), ((3, 2), first), ((2, 1), second), ((2, 3), second), ((2, 2), both)],
+        need(rows, cols),
+        need(cols + [(2, 0)], rows + [(0, 2)]),
+        [((a, b), ALL) for a in NEAR for b in NEAR],
+        need([(0, 2)] + far_rows, [(2, 0)] + far_cols),
+        need(far_cols, far_rows),
+        [((2, 2), (UP, GATE, HIGH_A, LOW_A, HIGH_B, LOW_B))],
     ]
-    done = [
-        [(0, 0)],
-        [],
-        [(1, 0), (3, 0), (0, 1), (0, 3)],
-        [(1, 1), (1, 3), (3, 1), (3, 3)],
-        [(2, 0), (0, 2)],
-        [(2, 1), (1, 2), (2, 3), (3, 2), (2, 2)],
-    ]
-    return waits, done
 
 
 def matmul(left, right):
@@ -101,8 +107,8 @@
 def fused_kernel(
     dims,
     x_hbm, ids_hbm, router_hbm, norms_hbm, rope_hbm, wq_hbm, wk_hbm, wv_hbm, wo_hbm, fg_hbm, fu_hbm, fd_hbm, eg_hbm, eu_hbm, ed_hbm,
-    out_hbm, gg_hbm, gu_hbm, gd_hbm,
-    xs, acc, gates, qs, ks, vs, os, s_outer, s_inner, p_outer, p_inner, tops, sums, ids, router, norms, rope, wqkv, wo, wg, wu, wd,
+    base_hbm, tokens_hbm, picks_hbm, shares_hbm, counts_hbm, gg_hbm, gu_hbm, gd_hbm,
+    picks, shares, counts, xs, acc, gates, qs, ks, vs, os, s_outer, s_inner, p_outer, p_inner, tops, sums, ids, router, norms, rope, wqkv, wo, wg, wu, wd,
     load_sem, w_sem, out_sem, ici_send, ici_recv, d2d_send, d2d_recv,
 ):
     rows, width, seq, hidden, heads, kv_heads, head = dims
@@ -110,7 +116,8 @@
     half = hidden // 2
     experts = 2 * len(BLOCKS)
     ffn_steps = fg_hbm.shape[1] // hidden
-    steps = ffn_steps + experts
+    steps = ffn_steps + STATIC
+    late = experts - STATIC
     me = lax.axis_index('ep')
     core = lax.rem(me, 2)
     col = lax.rem(me // 2, SIDE)
@@ -121,13 +128,19 @@
         cy = lax.rem(row + dy + SIDE, SIDE)
         return {'ep': (cy * SIDE + cx) * 2 + lax.rem(core + flip, 2)}
 
+    def cut(piece, gate, up, down):
+        if piece < LOW:
+            return (gate, up)[piece]
+        start, size = {LOW: (0, 2), HIGH: (2, 2), LOW_A: (0, 1), LOW_B: (1, 1), HIGH_A: (2, 1), HIGH_B: (3, 1)}[piece]
+        return down.at[pl.ds(start * hidden // 4, size * hidden // 4)]
+
     def piece_ref(block, piece):
         if block == 0:
-            return (eg_hbm.at[0], eu_hbm.at[0], ed_hbm.at[0, pl.ds(0, half)], ed_hbm.at[0, pl.ds(half, half)])[piece]
+            return cut(piece, eg_hbm.at[0], eu_hbm.at[0], ed_hbm.at[0])
         return slot_ref(2 * block, piece)
 
     def slot_ref(slot, piece):
-        return (gg_hbm.at[slot], gu_hbm.at[slot], gd_hbm.at[slot, pl.ds(0, half)], gd_hbm.at[slot, pl.ds(half, half)])[piece]
+        return cut(piece, gg_hbm.at[slot], gu_hbm.at[slot], gd_hbm.at[slot])
 
     def ici_copy(link, place, piece, source, target):
         return pltpu.make_async_remote_copy(
@@ -135,27 +148,33 @@
             send_sem=ici_send.at[link, place], recv_sem=ici_recv.at[target, piece],
             device_id=device(*STEPS[link], 0), device_id_type=pl.DeviceIdType.MESH)
 
-    def d2d_copies(block, own):
-        sources = (eg_hbm.at[0], eu_hbm.at[0], ed_hbm.at[0]) if own else (gg_hbm.at[2 * block], gu_hbm.at[2 * block], gd_hbm.at[2 * block])
-        targets = (gg_hbm.at[2 * block + 1], gu_hbm.at[2 * block + 1], gd_hbm.at[2 * block + 1])
-        return [pltpu.make_async_remote_copy(
-            src_ref=sources[k], dst_ref=targets[k], send_sem=d2d_send.at[block, k], recv_sem=d2d_recv.at[block, k],
-            device_id=device(0, 0, 1), device_id_type=pl.DeviceIdType.MESH) for k in range(3)]
+    def d2d_copy(block, piece, source):
+        return pltpu.make_async_remote_copy(
+            src_ref=source, dst_ref=slot_ref(2 * block + 1, piece), send_sem=d2d_send.at[block, piece], recv_sem=d2d_recv.at[block, piece],
+            device_id=device(0, 0, 1), device_id_type=pl.DeviceIdType.MESH)
+
+    def pieces_of(block):
+        return waits[-1][0][1] if block == len(BLOCKS) - 1 else ALL
+
+    def d2d_wait(block, pieces=ALL):
+        for piece in pieces:
+            d2d_copy(block, piece, slot_ref(2 * block + 1, piece)).wait_recv()
 
     plan = send_plan()
-    waits, done = wait_plan()
+    waits = wait_plan()
     arrival = {(target, piece): (link, place, piece, source, target) for stage in plan for link, place, piece, source, target in stage}
 
     def service(point):
-        for (dx, dy), pieces in waits[point]:
-            for piece in pieces:
-                ici_copy(*arrival[(block_of(dx, dy), piece)]).wait_recv()
+        landed = [(block_of(*block), piece) for block, pieces in waits[point] for piece in pieces]
+        for block, piece in landed:
+            ici_copy(*arrival[block, piece]).wait_recv()
+            if point >= len(plan):
+                d2d_copy(block, piece, piece_ref(block, piece)).start()
         if point < len(plan):
             for entry in plan[point]:
                 ici_copy(*entry).start()
-        for dx, dy in done[point]:
-            for copy in d2d_copies(block_of(dx, dy), (dx, dy) == (0, 0)):
-                copy.start()
+            for block, piece in landed if point else [(0, piece) for piece in ALL]:
+                d2d_copy(block, piece, piece_ref(block, piece)).start()
 
     loads = [
         (x_hbm, xs.at[1]), (norms_hbm, norms), (router_hbm, router), (ids_hbm, ids), (rope_hbm, rope),
@@ -193,8 +212,7 @@
 
             @pl.when(lax.rem(rank, 2) == 1)
             def _():
-                for copy in d2d_copies(rank // 2, False):
-                    copy.wait_recv()
+                d2d_wait(rank // 2)
 
             for copy in expert_copies(slot, (gg_hbm.at[rank], gu_hbm.at[rank], gd_hbm.at[rank])):
                 copy.start()
@@ -212,8 +230,17 @@
     ordered = (lax.broadcasted_iota(jnp.int32, (experts, experts), 1) == owner).astype(F32).astype(BF16)
     ordered = matmul(ordered, router[...]).astype(BF16)
     tile = 512
-
-    def prologue(index, carry):
+    tile_lanes = lax.broadcasted_iota(jnp.int32, (tile, LANES), 1)
+    spots = lax.broadcasted_iota(jnp.int32, (tile, tile), 1)
+    earlier = (lax.broadcasted_iota(jnp.int32, (tile, tile), 0) > spots).astype(F32).astype(BF16)
+    spots = spots.astype(F32)
+    quarters = tile // LANES
+    pitch = rows // LANES + 1
+    list_lines = (2 * tile + TILE) // LANES
+    picks[...] = jnp.zeros_like(picks)
+    shares[pl.ds(0, experts, stride=pitch), :] = jnp.zeros((experts, LANES), F32)
+
+    def prologue(index, so_far):
         part = pl.ds(pl.multiple_of(index * tile, tile), tile)
         values = xs[1, part, :].astype(F32)
         unit = values * norm_scale_of(values)
@@ -223,18 +250,44 @@
         acc[part, :] = values
         logits = matmul_t(ordered, tokens)
         per_seq = seq // tile
-        picks = ids[index // per_seq, :, pl.ds(pl.multiple_of(lax.rem(index, per_seq) * tile, tile), tile)]
-        picked = picks[0:1, :] == owner
-        for choice in range(1, picks.shape[0]):
-            picked = picked | (picks[choice:choice + 1, :] == owner)
+        wanted = ids[index // per_seq, :, pl.ds(pl.multiple_of(lax.rem(index, per_seq) * tile, tile), tile)]
+        picked = wanted[0:1, :] == owner
+        for choice in range(1, wanted.shape[0]):
+            picked = picked | (wanted[choice:choice + 1, :] == owner)
         top = jnp.max(jnp.where(picked, logits, -jnp.inf), axis=0, keepdims=True)
         powers = jnp.where(picked, jnp.exp(jnp.where(picked, logits, top) - top), 0.0)
         share = powers / jnp.sum(powers, axis=0, keepdims=True)
+        for lane_cut in range(quarters):
+            shares[pl.ds(1 + index * quarters + lane_cut, experts, stride=pitch), :] = share[:, lane_cut * LANES:(lane_cut + 1) * LANES]
         share = jnp.concatenate([share, jnp.zeros((LANES - experts, tile), F32)], axis=0)
-        gates[part, :] = share.T
-        return carry
-
-    lax.fori_loop(0, rows // tile, prologue, 0)
+        share = share.T
+        gates[part, :] = share
+
+        chosen = share > 0.0
+        ones = chosen.astype(F32)
+        place = jnp.where(chosen, matmul(earlier, ones.astype(BF16)) + so_far, -1.0)
+        so_far = so_far + jnp.sum(ones, axis=0, keepdims=True)
+        token = lax.broadcasted_iota(jnp.int32, (tile, tile), 0) + (index * tile + 1)
+        token = token.astype(F32)
+
+        def listed(rank, inner):
+            mine = tile_lanes == rank + STATIC
+            spot = jnp.sum(jnp.where(mine, place, 0.0), axis=1, keepdims=True)
+            for half in range(2):
+                found = jnp.sum(jnp.where(spot - half * tile == spots, token, 0.0), axis=0, keepdims=True).astype(jnp.int32)
+                for lane_cut in range(quarters):
+                    line = pl.ds(rank * list_lines + half * quarters + lane_cut, 1)
+                    picks[line, :] += found[:, lane_cut * LANES:(lane_cut + 1) * LANES]
+            return inner
+
+        lax.fori_loop(0, late, listed, 0)
+        return so_far
+
+    counts[...] = jnp.broadcast_to(lax.fori_loop(0, rows // tile, prologue, jnp.zeros((1, LANES), F32)), counts.shape).astype(jnp.int32)
+    results = [(xs.at[1], tokens_hbm), (picks, picks_hbm), (shares, shares_hbm), (counts, counts_hbm), (acc, base_hbm)]
+    results = [pltpu.make_async_copy(source, target, out_sem.at[k]) for k, (source, target) in enumerate(results)]
+    for copy in results[:-1]:
+        copy.start()
     for copy in loads[4:]:
         copy.wait()
 
@@ -345,7 +398,7 @@
 
     big = 1024
     lanes = lax.broadcasted_iota(jnp.int32, (big, LANES), 1)
-    moments = {ffn_steps // 2: 2, ffn_steps + 4: 3, ffn_steps + 11: 4, ffn_steps + 18: 5}
+    moments = {4: 2, 13: 3, 20: 4, 23: 5}
 
     def ffn_step(step, carry):
         slot = lax.rem(step, 2)
@@ -379,22 +432,131 @@
 
     lax.fori_loop(0, steps, ffn_step, 0)
 
-    def store(index):
-        part = pl.ds(index * tile, tile)
-        return pltpu.make_async_copy(xs.at[0, part], out_hbm.at[part], out_sem.at[index])
-
-    for index in range(rows // tile):
-        xs[0, index * tile:(index + 1) * tile, :] = acc[index * tile:(index + 1) * tile, :].astype(BF16)
-        store(index).start()
+    results[-1].start()
+    service(len(waits) - 1)
+    for block in range(STATIC // 2, len(BLOCKS)):
+        d2d_wait(block, pieces_of(block))
     for stage in plan:
         for entry in stage:
             ici_copy(*entry).wait_send()
     for block in range(len(BLOCKS)):
-        for copy in d2d_copies(block, block == 0):
-            copy.wait_send()
-    for index in range(rows // tile):
+        for piece in pieces_of(block):
+            d2d_copy(block, piece, piece_ref(block, piece)).wait_send()
+    for copy in results:
+        copy.wait()
+
+
+def compact_kernel(
+    dims,
+    picks_hbm, shares_hbm, counts_hbm, tokens_hbm, base_hbm, gg_hbm, gu_hbm, gd_hbm,
+    out_hbm,
+    picks, shares, counts, tokens, base, table, total, packed, lhs, result, wg, wu, wd,
+    load_sem, w_sem, out_sem,
+):
+    rows, width, first, ranks = dims
+    list_size = 1024 + TILE
+    parts = width // LANES
+    experts = first + ranks
+    loads = [pltpu.make_async_copy(source, target, load_sem.at[k]) for k, (source, target) in enumerate((
+        (tokens_hbm, tokens), (picks_hbm, picks), (shares_hbm, shares), (counts_hbm, counts), (base_hbm, base)))]
+    for copy in loads:
+        copy.start()
+
+    def weights(rank, slot):
+        return [pltpu.make_async_copy(source.at[first + rank], buffer.at[slot], w_sem.at[slot, k])
+                for k, (source, buffer) in enumerate(((gg_hbm, wg), (gu_hbm, wu), (gd_hbm, wd)))]
+
+    for copy in weights(0, 0):
+        copy.start()
+
+    loads[0].wait()
+    table[0] = jnp.zeros((parts, LANES), F32)
+    total[0] = jnp.zeros((parts, LANES), F32)
+    flat = table.reshape((rows + 1) * parts, LANES)
+    step_rows = 512
+
+    def spread(index, carry):
+        start = pl.multiple_of(index * step_rows, step_rows)
+        values = tokens[pl.ds(start, step_rows), :].astype(F32)
+        for part in range(parts):
+            flat[pl.ds(parts + start * parts + part, step_rows, stride=parts), :] = values[:, part * LANES:(part + 1) * LANES]
+        total[pl.ds(1 + start, step_rows)] = jnp.zeros((step_rows, parts, LANES), F32)
+        return carry
+
+    lax.fori_loop(0, rows // step_rows, spread, 0)
+    for copy in loads[1:4]:
+        copy.wait()
+
+    def tiles_of(rank):
+        return jnp.maximum((counts[0, first + rank] + TILE - 1) // TILE, 1)
+
+    lot = rows + LANES
+
+    def gather(rank, tile):
+        start = rank * list_size + tile * TILE
+        for place in range(TILE):
+            spots = pl.ds(place // UNIT * UNIT * parts + place % UNIT, parts, stride=UNIT)
+            packed.reshape(TILE * parts, LANES)[spots, :] = table[picks[start + place]]
+
+    def scatter(rank, tile):
+        start = rank * list_size + tile * TILE
+        lead = (first + rank) * lot + LANES - 1
+        for group in range(0, TILE, UNIT):
+            rows_of = [picks[start + group + place] for place in range(UNIT)]
+            sums = [total[row] + shares[lead + row] * result[group + place] for place, row in enumerate(rows_of)]
+            for row, value in zip(rows_of, sums):
+                total[row] = value
+
+    count = lax.fori_loop(0, ranks, lambda rank, so_far: so_far + tiles_of(rank), 0)
+    gather(0, 0)
+
+    def tile_step(index, carry):
+        rank, tile, last_rank, last_tile = carry
+        slot = lax.rem(rank, 2)
+
+        @pl.when(tile == 0)
+        def _():
+            for copy in weights(rank, slot):
+                copy.wait()
+
+            @pl.when(rank + 1 < ranks)
+            def _():
+                for copy in weights(rank + 1, 1 - slot):
+                    copy.start()
+
+        more = tile + 1 < tiles_of(rank)
+        next_rank = jnp.where(more, rank, rank + 1)
+        next_tile = jnp.where(more, tile + 1, 0)
+        for part in range(parts):
+            lhs[:, part * LANES:(part + 1) * LANES] = packed[:, part].reshape(TILE, LANES).astype(BF16)
+        scatter(last_rank, last_tile)
+        gather(next_rank, next_tile)
+        gate_act = matmul(lhs[...], wg[slot])
+        up_act = matmul(lhs[...], wu[slot])
+        mixed = (jax.nn.silu(gate_act) * up_act).astype(BF16)
+        down = matmul(mixed, wd[slot]).astype(BF16).astype(F32)
+        for part in range(parts):
+            result.reshape(TILE * parts, LANES)[pl.ds(part, TILE, stride=parts), :] = down[:, part * LANES:(part + 1) * LANES]
+        return next_rank, next_tile, rank, tile
+
+    _, _, last_rank, last_tile = lax.fori_loop(0, count, tile_step, (jnp.int32(0), jnp.int32(0), jnp.int32(ranks), jnp.int32(0)))
+    scatter(last_rank, last_tile)
+    loads[4].wait()
+    sums_of = total.reshape((rows + 1) * parts, LANES)
+
+    def store(index):
+        part = pl.ds(index * step_rows, step_rows)
+        return pltpu.make_async_copy(tokens.at[part], out_hbm.at[part], out_sem.at[index])
+
+    for index in range(rows // step_rows):
+        span = slice(index * step_rows, (index + 1) * step_rows)
+        for part in range(parts):
+            cols = slice(part * LANES, (part + 1) * LANES)
+            moe = sums_of[pl.ds(parts + index * step_rows * parts + part, step_rows, stride=parts), :]
+            tokens[span, cols] = (base[span, cols] + moe).astype(BF16)
+        store(index).start()
+    for index in range(rows // step_rows):
         store(index).wait()
-
 
 def rope_tables(seq, head):
     half = head // 2
@@ -432,23 +594,26 @@
             w_value.transpose(1, 2, 0).reshape(kv_heads * head, width), w_out.reshape(heads * head, width),
             w_gate, w_up, w_down, expert_gate, expert_up, expert_down)
         flops = rows * width * 2 * (3 * hidden * experts + 3 * w_gate.shape[1] + 3 * heads * head)
-        out = pl.pallas_call(
+        late = experts - STATIC
+        lists = ((late + 1) * (1024 + TILE) // LANES, LANES)
+        lots = (experts * (rows // LANES + 1), LANES)
+        weight_shapes = ((width, hidden), (width, hidden), (hidden, width))
+        double = [pltpu.VMEM((2,) + shape, BF16) for shape in weight_shapes]
+        base, tokens, picks, shares, counts, gate_all, up_all, down_all = pl.pallas_call(
             functools.partial(fused_kernel, (rows, width, seq, hidden, heads, kv_heads, head)),
-            out_shape=(
-                jax.ShapeDtypeStruct((rows, width), BF16),
-                jax.ShapeDtypeStruct((experts, width, hidden), BF16),
-                jax.ShapeDtypeStruct((experts, width, hidden), BF16),
-                jax.ShapeDtypeStruct((experts, hidden, width), BF16)),
+            out_shape=tuple(jax.ShapeDtypeStruct(shape, kind) for shape, kind in (
+                ((rows, width), F32), ((rows, width), BF16), (lists, jnp.int32), (lots, F32), ((UNIT, LANES), jnp.int32),
+                *[((experts,) + shape, BF16) for shape in weight_shapes])),
             in_specs=[anywhere] * len(operands),
-            out_specs=[anywhere] * 4,
+            out_specs=[anywhere] * 8,
             scratch_shapes=[
+                pltpu.VMEM(lists, jnp.int32),
+                pltpu.VMEM(lots, F32),
+                pltpu.VMEM((UNIT, LANES), jnp.int32),
                 pltpu.VMEM((2, rows, width), BF16),
                 pltpu.VMEM((rows, width), F32),
                 pltpu.VMEM((rows, LANES), F32),
-                pltpu.VMEM((seq, heads * head), BF16),
-                pltpu.VMEM((seq, kv_heads * LANES), BF16),
-                pltpu.VMEM((seq, kv_heads * LANES), BF16),
-                pltpu.VMEM((seq, heads * head), BF16),
+                *[pltpu.VMEM((seq, heads * head), BF16) for _ in range(4)],
                 *[pltpu.VMEM((512, 1280), kind) for kind in (F32, F32, BF16, BF16)],
                 *[pltpu.VMEM((4, 512, LANES), F32) for _ in range(2)],
                 pltpu.VMEM((micro * seqs, choices, seq), jnp.int32),
@@ -457,12 +622,35 @@
                 pltpu.VMEM((2, seq, LANES), F32),
                 pltpu.VMEM((4, 512, width), BF16),
                 pltpu.VMEM((2, 512, width), BF16),
-                *[pltpu.VMEM((2,) + shape, BF16) for shape in ((width, hidden), (width, hidden), (hidden, width))],
-                *[pltpu.SemaphoreType.DMA(shape) for shape in ((11,), (2, 3), (4,), (4, 15), (16, 4), (16, 3), (16, 3))],
+                *double,
+                *[pltpu.SemaphoreType.DMA(shape) for shape in ((11,), (2, 3), (5,), (4, 16), (16, 8), (16, 8), (16, 8))],
             ],
             compiler_params=pltpu.CompilerParams(collective_id=0, has_side_effects=True, vmem_limit_bytes=62 * 1024 * 1024),
             cost_estimate=pl.CostEstimate(flops=flops, bytes_accessed=experts * 6 * width * hidden, transcendentals=0),
-        )(*operands)[0]
+        )(*operands)
+        parts = width // LANES
+        picks, shares = picks.reshape(-1), shares.reshape(-1)
+        staged = pltpu.VMEM((TILE // UNIT, parts, UNIT, LANES), F32)
+        out = pl.pallas_call(
+            functools.partial(compact_kernel, (rows, width, STATIC, late)),
+            out_shape=jax.ShapeDtypeStruct((rows, width), BF16),
+            in_specs=[anywhere] * 8,
+            out_specs=anywhere,
+            scratch_shapes=[
+                pltpu.SMEM((picks.size,), jnp.int32),
+                pltpu.SMEM((shares.size,), F32),
+                pltpu.SMEM((UNIT, LANES), jnp.int32),
+                pltpu.VMEM((rows, width), BF16),
+                pltpu.VMEM((rows, width), F32),
+                *[pltpu.VMEM((rows + 1, parts, LANES), F32) for _ in range(2)],
+                staged,
+                pltpu.VMEM((TILE, width), BF16),
+                pltpu.VMEM((TILE, parts, LANES), F32),
+                *double,
+                *[pltpu.SemaphoreType.DMA(shape) for shape in ((5,), (2, 3), (4,))],
+            ],
+            compiler_params=pltpu.CompilerParams(vmem_limit_bytes=62 * 1024 * 1024),
+        )(picks, shares, counts, tokens, base, gate_all, up_all, down_all)
         return out.reshape(resid_in.shape)
 
     return jax.shard_map(local_program, mesh=mesh, in_specs=(tok_spec, tok_spec, tok_spec, rep_three, rep_three, rep_three, rep_three, rep_two, rep_two, rep_two, rep_two, rep_one, rep_one, rep_one, expert_spec, expert_spec, expert_spec), out_specs=tok_spec, check_vma=False)

time: 384 us -> 360 us (0.938)
  the two profiles are of different devices: /device:TPU:107 before, /device:TPU:100 now
where the time goes in v3:
time: 360 us; the launch traced here: 355 us
  Pallas kernels  352 us (98%)
    pallas_call x1, Pallas kernels, local_program(): pl.pallas_call(functools.partial(fused_kernel, (rows, width, seq, hidden,...  275 us
    pallas_call x1, Pallas kernels, local_program(): pl.pallas_call(functools.partial(compact_kernel, (rows, width, STATIC, la...  76.5 us

profile of v3, /device:TPU:100, one launch (start us, length us, event | category | flops | bytes accessed | tf_op | source)
XLA Modules:
  0.0 354.8 jit_solution(16492243956713643490)
XLA Ops:
  0.0 0.7 stack.12
  0.7 0.7 stack.13
  1.4 0.7 stack.14
  2.1 0.6 maximum_convert_fusion.norms_hbm
  2.7 275.5 %shard_map.163 = (f32[2048,1024]{1,0:T(8,128)}, bf16[2048,1024]{1,0:T(8,128)(2,1)}, s32[170,128]{1,0:T(8,128)}, f32[544,128]{1,0:T(8,128)}, s32[8,128]{1,0:T(8,1...) custom-call(bf16[2048,1024]{1,0:T(8,128)(2,1)} %bitcast.24, ...), custom_call_target="tpu_custom_call" | custom-call | flops 270582939648 | bytes 100663296 | tf_op jit(solution)/shard_map/pallas_call | solution.py:602
  278.2 76.5 %shard_map.164 = bf16[2048,1024]{1,0:T(8,128)(2,1)} custom-call(s32[21760]{0:T(1024)} %bitcast.23, f32[69632]{0:T(1024)} %bitcast.22, s32[8,128]{1,0:T(8,128)} %get-tuple-element.15.counts_hbm, bf16[2048,1024]{1,0:T(8,128)(2,1)} %get-tuple-element.16.tokens_hbm, f32[2048,1024]{1,0:T(8,128)} %get-tuple-element.17.base_hbm, ...), custom_call_target="tpu_custom_call" | custom-call | tf_op jit(solution)/shard_map/pallas_call | solution.py:634

commit v4 on v3

--- a/solution.py
+++ b/solution.py
@@ -17,7 +17,7 @@
 
 UNIT = 8
 TILE = 256
-STATIC = 16
+STATIC = 18
 
 SIDE = 4
 NEAR = (1, 3)
@@ -87,8 +87,8 @@
         need(cols + [(2, 0)], rows + [(0, 2)]),
         [((a, b), ALL) for a in NEAR for b in NEAR],
         need([(0, 2)] + far_rows, [(2, 0)] + far_cols),
-        need(far_cols, far_rows),
-        [((2, 2), (UP, GATE, HIGH_A, LOW_A, HIGH_B, LOW_B))],
+        [((2, 1), Y_FIRST), ((1, 2), X_FIRST), ((2, 3), (HIGH,)), ((3, 2), (LOW,))],
+        [((2, 3), (UP,)), ((3, 2), (GATE,)), ((2, 2), (UP, GATE, HIGH_A, LOW_A, HIGH_B, LOW_B))],
     ]
 
 
@@ -106,9 +106,9 @@
 
 def fused_kernel(
     dims,
-    x_hbm, ids_hbm, router_hbm, norms_hbm, rope_hbm, wq_hbm, wk_hbm, wv_hbm, wo_hbm, fg_hbm, fu_hbm, fd_hbm, eg_hbm, eu_hbm, ed_hbm,
+    x_hbm, ids_hbm, router_hbm, na_hbm, nf_hbm, nm_hbm, rope_hbm, wq_hbm, wk_hbm, wv_hbm, wo_hbm, fg_hbm, fu_hbm, fd_hbm, eg_hbm, eu_hbm, ed_hbm,
     base_hbm, tokens_hbm, picks_hbm, shares_hbm, counts_hbm, gg_hbm, gu_hbm, gd_hbm,
-    picks, shares, counts, xs, acc, gates, qs, ks, vs, os, s_outer, s_inner, p_outer, p_inner, tops, sums, ids, router, norms, rope, wqkv, wo, wg, wu, wd,
+    picks, shares, lots, counts, xs, acc, gates, qs, ks, vs, os, s_outer, s_inner, p_outer, p_inner, tops, sums, ids, router, na, nf, nm, rope, wqkv, wo, wg, wu, wd,
     load_sem, w_sem, out_sem, ici_send, ici_recv, d2d_send, d2d_recv,
 ):
     rows, width, seq, hidden, heads, kv_heads, head = dims
@@ -154,7 +154,7 @@
             device_id=device(0, 0, 1), device_id_type=pl.DeviceIdType.MESH)
 
     def pieces_of(block):
-        return waits[-1][0][1] if block == len(BLOCKS) - 1 else ALL
+        return waits[-1][-1][1] if block == len(BLOCKS) - 1 else ALL
 
     def d2d_wait(block, pieces=ALL):
         for piece in pieces:
@@ -177,7 +177,7 @@
                 d2d_copy(block, piece, piece_ref(block, piece)).start()
 
     loads = [
-        (x_hbm, xs.at[1]), (norms_hbm, norms), (router_hbm, router), (ids_hbm, ids), (rope_hbm, rope),
+        (x_hbm, xs.at[1]), (na_hbm, na), (nf_hbm, nf), (nm_hbm, nm), (router_hbm, router), (ids_hbm, ids), (rope_hbm, rope),
         (wq_hbm.at[pl.ds(0, 512)], wqkv.at[0]), (wq_hbm.at[pl.ds(512, 512)], wqkv.at[1]), (wk_hbm, wqkv.at[2]), (wv_hbm, wqkv.at[3]),
         (wo_hbm.at[pl.ds(0, 512)], wo.at[0]), (wo_hbm.at[pl.ds(512, 512)], wo.at[1]),
     ]
@@ -219,8 +219,9 @@
 
     prefetch(0, 0)
 
-    for copy in loads[:4]:
+    for copy in loads[:6]:
         copy.wait()
+    norm_attn, norm_ffn, norm_moe = [scale[...].astype(F32).reshape(1, width) for scale in (na, nf, nm)]
     ranks = lax.broadcasted_iota(jnp.int32, (experts, 1), 0)
     owner = jnp.zeros((experts, 1), jnp.int32)
     for block, (dx, dy) in enumerate(BLOCKS):
@@ -235,17 +236,16 @@
     earlier = (lax.broadcasted_iota(jnp.int32, (tile, tile), 0) > spots).astype(F32).astype(BF16)
     spots = spots.astype(F32)
     quarters = tile // LANES
-    pitch = rows // LANES + 1
-    list_lines = (2 * tile + TILE) // LANES
+    list_lines = (rows // 2 + TILE) // LANES
     picks[...] = jnp.zeros_like(picks)
-    shares[pl.ds(0, experts, stride=pitch), :] = jnp.zeros((experts, LANES), F32)
-
-    def prologue(index, so_far):
+    shares[...] = jnp.zeros_like(shares)
+
+    def prologue(halves, index, so_far):
         part = pl.ds(pl.multiple_of(index * tile, tile), tile)
         values = xs[1, part, :].astype(F32)
         unit = values * norm_scale_of(values)
-        tokens = (unit * norms[2:3, :]).astype(BF16)
-        xs[0, part, :] = (unit * norms[0:1, :]).astype(BF16)
+        tokens = (unit * norm_moe).astype(BF16)
+        xs[0, part, :] = (unit * norm_attn).astype(BF16)
         xs[1, part, :] = tokens
         acc[part, :] = values
         logits = matmul_t(ordered, tokens)
@@ -257,8 +257,7 @@
         top = jnp.max(jnp.where(picked, logits, -jnp.inf), axis=0, keepdims=True)
         powers = jnp.where(picked, jnp.exp(jnp.where(picked, logits, top) - top), 0.0)
         share = powers / jnp.sum(powers, axis=0, keepdims=True)
-        for lane_cut in range(quarters):
-            shares[pl.ds(1 + index * quarters + lane_cut, experts, stride=pitch), :] = share[:, lane_cut * LANES:(lane_cut + 1) * LANES]
+        lots[...] = share
         share = jnp.concatenate([share, jnp.zeros((LANES - experts, tile), F32)], axis=0)
         share = share.T
         gates[part, :] = share
@@ -267,28 +266,39 @@
         ones = chosen.astype(F32)
         place = jnp.where(chosen, matmul(earlier, ones.astype(BF16)) + so_far, -1.0)
         so_far = so_far + jnp.sum(ones, axis=0, keepdims=True)
-        token = lax.broadcasted_iota(jnp.int32, (tile, tile), 0) + (index * tile + 1)
-        token = token.astype(F32)
+        token = lax.broadcasted_iota(jnp.int32, (1, tile), 1) + (index * tile + 1)
+        major, minor = (token // TILE).astype(F32), lax.rem(token, TILE).astype(F32)
 
         def listed(rank, inner):
-            mine = tile_lanes == rank + STATIC
-            spot = jnp.sum(jnp.where(mine, place, 0.0), axis=1, keepdims=True)
-            for half in range(2):
-                found = jnp.sum(jnp.where(spot - half * tile == spots, token, 0.0), axis=0, keepdims=True).astype(jnp.int32)
+            spot = jnp.sum(jnp.where(tile_lanes == rank + STATIC, place, 0.0), axis=1, keepdims=True)
+            weight = lots[pl.ds(rank + STATIC, 1), :]
+            high = weight.astype(BF16).astype(F32)
+            middle = (weight - high).astype(BF16).astype(F32)
+            facts = jnp.concatenate([major, minor, high, middle, weight - high - middle, jnp.zeros((3, tile), F32)], axis=0).astype(BF16)
+            for half in range(halves):
+                found = matmul(facts, jnp.where(spot - half * tile == spots, 1.0, 0.0).astype(BF16))
+                row = (found[0:1] * TILE + found[1:2]).astype(jnp.int32)
+                share_row = found[2:3] + found[3:4] + found[4:5]
                 for lane_cut in range(quarters):
                     line = pl.ds(rank * list_lines + half * quarters + lane_cut, 1)
-                    picks[line, :] += found[:, lane_cut * LANES:(lane_cut + 1) * LANES]
+                    lane_span = slice(lane_cut * LANES, (lane_cut + 1) * LANES)
+                    picks[line, :] += row[:, lane_span]
+                    shares[line, :] += share_row[:, lane_span]
             return inner
 
         lax.fori_loop(0, late, listed, 0)
         return so_far
 
-    counts[...] = jnp.broadcast_to(lax.fori_loop(0, rows // tile, prologue, jnp.zeros((1, LANES), F32)), counts.shape).astype(jnp.int32)
+    taken = jnp.zeros((1, LANES), F32)
+    for micro_index in range(micro):
+        first_tile = micro_index * seq // tile
+        taken = lax.fori_loop(first_tile, first_tile + seq // tile, functools.partial(prologue, micro_index + 1), taken)
+    counts[...] = jnp.broadcast_to(taken, counts.shape).astype(jnp.int32)
     results = [(xs.at[1], tokens_hbm), (picks, picks_hbm), (shares, shares_hbm), (counts, counts_hbm), (acc, base_hbm)]
     results = [pltpu.make_async_copy(source, target, out_sem.at[k]) for k, (source, target) in enumerate(results)]
     for copy in results[:-1]:
         copy.start()
-    for copy in loads[4:]:
+    for copy in loads[6:]:
         copy.wait()
 
     def sequence(micro_index, carry):
@@ -388,7 +398,7 @@
             added = matmul(os[local, :tile], wo[0]) + matmul(os[local, tile:], wo[1])
             after = (acc[part, :] + added).astype(BF16).astype(F32)
             acc[part, :] = after
-            xs[0, part, :] = (after * norm_scale_of(after) * norms[1:2, :]).astype(BF16)
+            xs[0, part, :] = (after * norm_scale_of(after) * norm_ffn).astype(BF16)
             return inner
 
         lax.fori_loop(0, seq // tile, project, 0)
@@ -398,39 +408,38 @@
 
     big = 1024
     lanes = lax.broadcasted_iota(jnp.int32, (big, LANES), 1)
-    moments = {4: 2, 13: 3, 20: 4, 23: 5}
-
-    def ffn_step(step, carry):
+    moments = {5: 2, 14: 3, 21: 4, 24: 5}
+
+    def ffn_step(dense, step, carry):
         slot = lax.rem(step, 2)
         for copy in expert_copies(slot, (gg_hbm.at[0], gu_hbm.at[0], gd_hbm.at[0])):
             copy.wait()
         for moment, point in moments.items():
-            @pl.when(step == moment)
-            def _():
-                service(point)
+            if dense == (moment < ffn_steps):
+                @pl.when(step == moment)
+                def _():
+                    service(point)
 
         prefetch(step + 1, 1 - slot)
-        dense = step < ffn_steps
-        source = (step + steps - ffn_steps) // steps
         gate_w, up_w, down_w = wg.at[slot], wu.at[slot], wd.at[slot]
 
         def rows_step(index, inner):
             part = pl.ds(pl.multiple_of(index * big, big), big)
-            tokens = xs[source, part, :]
-            weight = jnp.sum(jnp.where(lanes == step - ffn_steps, gates[part, :], 0.0), axis=1, keepdims=True)
-            weight = jnp.where(dense, 1.0, weight)
-            gate_act = matmul(tokens, gate_w[...])
-            up_act = matmul(tokens, up_w[...])
-            mixed = (jax.nn.silu(gate_act) * up_act).astype(BF16)
-            down = matmul(mixed, down_w[...])
-            down = jnp.where(dense, down, down.astype(BF16).astype(F32))
-            acc[part, :] += jnp.where(weight > 0.0, weight * down, 0.0)
+            tokens = xs[0 if dense else 1, part, :]
+            mixed = jax.nn.silu(matmul(tokens, gate_w[...])) * matmul(tokens, up_w[...])
+            if dense:
+                acc[part, :] += matmul(mixed.astype(BF16), down_w[...])
+            else:
+                weight = jnp.sum(jnp.where(lanes == step - ffn_steps, gates[part, :], 0.0), axis=1, keepdims=True)
+                mixed = jnp.where(weight > 0.0, mixed, 0.0).astype(BF16)
+                acc[part, :] += weight * matmul(mixed, down_w[...]).astype(BF16).astype(F32)
             return inner
 
         lax.fori_loop(0, rows // big, rows_step, 0)
         return carry
 
-    lax.fori_loop(0, steps, ffn_step, 0)
+    lax.fori_loop(0, ffn_steps, functools.partial(ffn_step, True), 0)
+    lax.fori_loop(ffn_steps, steps, functools.partial(ffn_step, False), 0)
 
     results[-1].start()
     service(len(waits) - 1)
@@ -454,7 +463,7 @@
     load_sem, w_sem, out_sem,
 ):
     rows, width, first, ranks = dims
-    list_size = 1024 + TILE
+    list_size = rows // 2 + TILE
     parts = width // LANES
     experts = first + ranks
     loads = [pltpu.make_async_copy(source, target, load_sem.at[k]) for k, (source, target) in enumerate((
@@ -490,8 +499,6 @@
     def tiles_of(rank):
         return jnp.maximum((counts[0, first + rank] + TILE - 1) // TILE, 1)
 
-    lot = rows + LANES
-
     def gather(rank, tile):
         start = rank * list_size + tile * TILE
         for place in range(TILE):
@@ -500,12 +507,16 @@
 
     def scatter(rank, tile):
         start = rank * list_size + tile * TILE
-        lead = (first + rank) * lot + LANES - 1
         for group in range(0, TILE, UNIT):
             rows_of = [picks[start + group + place] for place in range(UNIT)]
-            sums = [total[row] + shares[lead + row] * result[group + place] for place, row in enumerate(rows_of)]
+            sums = [total[row] + result[group + place] for place, row in enumerate(rows_of)]
             for row, value in zip(rows_of, sums):
                 total[row] = value
+
+    def factor(rank, tile):
+        line = (rank * list_size + tile * TILE) // LANES
+        lines = [jnp.broadcast_to(shares[pl.ds(line + k, 1), :], (LANES, LANES)).T for k in range(TILE // LANES)]
+        return jnp.concatenate(lines, axis=0)
 
     count = lax.fori_loop(0, ranks, lambda rank, so_far: so_far + tiles_of(rank), 0)
     gather(0, 0)
@@ -535,8 +546,9 @@
         up_act = matmul(lhs[...], wu[slot])
         mixed = (jax.nn.silu(gate_act) * up_act).astype(BF16)
         down = matmul(mixed, wd[slot]).astype(BF16).astype(F32)
+        share = factor(rank, tile)
         for part in range(parts):
-            result.reshape(TILE * parts, LANES)[pl.ds(part, TILE, stride=parts), :] = down[:, part * LANES:(part + 1) * LANES]
+            result.reshape(TILE * parts, LANES)[pl.ds(part, TILE, stride=parts), :] = share * down[:, part * LANES:(part + 1) * LANES]
         return next_rank, next_tile, rank, tile
 
     _, _, last_rank, last_tile = lax.fori_loop(0, count, tile_step, (jnp.int32(0), jnp.int32(0), jnp.int32(ranks), jnp.int32(0)))
@@ -585,30 +597,30 @@
         experts = 2 * len(BLOCKS)
         rows = micro * seqs * seq
         ids = expert_idx.transpose(0, 1, 3, 2).reshape(micro * seqs, choices, seq)
-        norms = jnp.stack([norm_attn, norm_ffn, norm_moe]).astype(F32)
         rope = jnp.asarray(rope_tables(seq, head))
         anywhere = pl.BlockSpec(memory_space=pl.ANY)
         operands = (
-            resid_in.reshape(rows, width), ids, w_router.T, norms, rope,
+            resid_in.reshape(rows, width), ids, w_router.T, norm_attn, norm_ffn, norm_moe, rope,
             w_query.transpose(1, 2, 0).reshape(heads * head, width), w_key.transpose(1, 2, 0).reshape(kv_heads * head, width),
             w_value.transpose(1, 2, 0).reshape(kv_heads * head, width), w_out.reshape(heads * head, width),
             w_gate, w_up, w_down, expert_gate, expert_up, expert_down)
         flops = rows * width * 2 * (3 * hidden * experts + 3 * w_gate.shape[1] + 3 * heads * head)
         late = experts - STATIC
-        lists = ((late + 1) * (1024 + TILE) // LANES, LANES)
-        lots = (experts * (rows // LANES + 1), LANES)
+        list_size = rows // 2 + TILE
+        lists = ((late + 1) * list_size // LANES, LANES)
         weight_shapes = ((width, hidden), (width, hidden), (hidden, width))
         double = [pltpu.VMEM((2,) + shape, BF16) for shape in weight_shapes]
         base, tokens, picks, shares, counts, gate_all, up_all, down_all = pl.pallas_call(
             functools.partial(fused_kernel, (rows, width, seq, hidden, heads, kv_heads, head)),
             out_shape=tuple(jax.ShapeDtypeStruct(shape, kind) for shape, kind in (
-                ((rows, width), F32), ((rows, width), BF16), (lists, jnp.int32), (lots, F32), ((UNIT, LANES), jnp.int32),
+                ((rows, width), F32), ((rows, width), BF16), (lists, jnp.int32), (lists, F32), ((UNIT, LANES), jnp.int32),
                 *[((experts,) + shape, BF16) for shape in weight_shapes])),
             in_specs=[anywhere] * len(operands),
             out_specs=[anywhere] * 8,
             scratch_shapes=[
                 pltpu.VMEM(lists, jnp.int32),
-                pltpu.VMEM(lots, F32),
+                pltpu.VMEM(lists, F32),
+                pltpu.VMEM((experts, 512), F32),
                 pltpu.VMEM((UNIT, LANES), jnp.int32),
                 pltpu.VMEM((2, rows, width), BF16),
                 pltpu.VMEM((rows, width), F32),
@@ -618,18 +630,18 @@
                 *[pltpu.VMEM((4, 512, LANES), F32) for _ in range(2)],
                 pltpu.VMEM((micro * seqs, choices, seq), jnp.int32),
                 pltpu.VMEM((experts, width), BF16),
-                pltpu.VMEM((3, width), F32),
+                *[pltpu.VMEM((width,), BF16) for _ in range(3)],
                 pltpu.VMEM((2, seq, LANES), F32),
                 pltpu.VMEM((4, 512, width), BF16),
                 pltpu.VMEM((2, 512, width), BF16),
                 *double,
-                *[pltpu.SemaphoreType.DMA(shape) for shape in ((11,), (2, 3), (5,), (4, 16), (16, 8), (16, 8), (16, 8))],
+                *[pltpu.SemaphoreType.DMA(shape) for shape in ((13,), (2, 3), (5,), (4, 16), (16, 8), (16, 8), (16, 8))],
             ],
             compiler_params=pltpu.CompilerParams(collective_id=0, has_side_effects=True, vmem_limit_bytes=62 * 1024 * 1024),
             cost_estimate=pl.CostEstimate(flops=flops, bytes_accessed=experts * 6 * width * hidden, transcendentals=0),
         )(*operands)
         parts = width // LANES
-        picks, shares = picks.reshape(-1), shares.reshape(-1)
+        picks = picks.reshape(-1)
         staged = pltpu.VMEM((TILE // UNIT, parts, UNIT, LANES), F32)
         out = pl.pallas_call(
             functools.partial(compact_kernel, (rows, width, STATIC, late)),
@@ -638,7 +650,7 @@
             out_specs=anywhere,
             scratch_shapes=[
                 pltpu.SMEM((picks.size,), jnp.int32),
-                pltpu.SMEM((shares.size,), F32),
+                pltpu.VMEM(lists, F32),
                 pltpu.SMEM((UNIT, LANES), jnp.int32),
                 pltpu.VMEM((rows, width), BF16),
                 pltpu.VMEM((rows, width), F32),

time: 360 us -> 352 us (0.978)
  the two profiles are of different devices: /device:TPU:100 before, /device:TPU:107 now
where the time goes in v4:
time: 352 us; the launch traced here: 351 us
  Pallas kernels  350 us (99%)
    pallas_call x1, Pallas kernels, local_program(): pl.pallas_call(functools.partial(fused_kernel, (rows, width, seq, hidden,...  278 us
    pallas_call x1, Pallas kernels, local_program(): pl.pallas_call(functools.partial(compact_kernel, (rows, width, STATIC, la...  72.5 us

profile of v4, /device:TPU:107, one launch (start us, length us, event | category | flops | bytes accessed | tf_op | source)
XLA Modules:
  0.0 350.5 jit_solution(14430512588073303156)
XLA Ops:
  0.0 277.9 %shard_map.163 = (f32[2048,1024]{1,0:T(8,128)}, bf16[2048,1024]{1,0:T(8,128)(2,1)}, s32[150,128]{1,0:T(8,128)}, f32[150,128]{1,0:T(8,128)}, s32[8,128]{1,0:T(8,1...) custom-call(bf16[2048,1024]{1,0:T(8,128)(2,1)} %bitcast.22, ...), custom_call_target="tpu_custom_call" | custom-call | flops 270582939648 | bytes 100663296 | tf_op jit(solution)/shard_map/pallas_call | solution.py:613
  277.9 72.5 %shard_map.164 = bf16[2048,1024]{1,0:T(8,128)(2,1)} custom-call(s32[19200]{0:T(1024)} %bitcast.21, f32[150,128]{1,0:T(8,128)} %get-tuple-element.14.shares_hbm, s32[8,128]{1,0:T(8,128)} %get-tuple-element.15.counts_hbm, bf16[2048,1024]{1,0:T(8,128)(2,1)} %get-tuple-element.16.tokens_hbm, f32[2048,1024]{1,0:T(8,128)} %get-tuple-element.17.base_hbm, ...), custom_call_target="tpu_custom_call" | custom-call | tf_op jit(solution)/shard_map/pallas_call | solution.py:646

commit v5 on v4

--- a/solution.py
+++ b/solution.py
@@ -435,7 +435,11 @@
                 acc[part, :] += weight * matmul(mixed, down_w[...]).astype(BF16).astype(F32)
             return inner
 
-        lax.fori_loop(0, rows // big, rows_step, 0)
+        if dense:
+            lax.fori_loop(0, rows // big, rows_step, 0)
+        else:
+            for index in range(rows // big):
+                rows_step(index, 0)
         return carry
 
     lax.fori_loop(0, ffn_steps, functools.partial(ffn_step, True), 0)
@@ -502,14 +506,13 @@
     def gather(rank, tile):
         start = rank * list_size + tile * TILE
         for place in range(TILE):
-            spots = pl.ds(place // UNIT * UNIT * parts + place % UNIT, parts, stride=UNIT)
-            packed.reshape(TILE * parts, LANES)[spots, :] = table[picks[start + place]]
+            packed[place] = table[picks[start + place]]
 
     def scatter(rank, tile):
         start = rank * list_size + tile * TILE
         for group in range(0, TILE, UNIT):
             rows_of = [picks[start + group + place] for place in range(UNIT)]
-            sums = [total[row] + result[group + place] for place, row in enumerate(rows_of)]
+            sums = [total[row] + result.reshape(TILE * parts, LANES)[pl.ds(group * parts + place, parts, stride=UNIT), :] for place, row in enumerate(rows_of)]
             for row, value in zip(rows_of, sums):
                 total[row] = value
 
@@ -539,7 +542,7 @@
         next_rank = jnp.where(more, rank, rank + 1)
         next_tile = jnp.where(more, tile + 1, 0)
         for part in range(parts):
-            lhs[:, part * LANES:(part + 1) * LANES] = packed[:, part].reshape(TILE, LANES).astype(BF16)
+            lhs[:, part * LANES:(part + 1) * LANES] = packed.reshape(TILE * parts, LANES)[pl.ds(part, TILE, stride=parts), :].astype(BF16)
         scatter(last_rank, last_tile)
         gather(next_rank, next_tile)
         gate_act = matmul(lhs[...], wg[slot])
@@ -548,7 +551,7 @@
         down = matmul(mixed, wd[slot]).astype(BF16).astype(F32)
         share = factor(rank, tile)
         for part in range(parts):
-            result.reshape(TILE * parts, LANES)[pl.ds(part, TILE, stride=parts), :] = share * down[:, part * LANES:(part + 1) * LANES]
+            result[:, part] = (share * down[:, part * LANES:(part + 1) * LANES]).reshape(TILE // UNIT, UNIT, LANES)
         return next_rank, next_tile, rank, tile
 
     _, _, last_rank, last_tile = lax.fori_loop(0, count, tile_step, (jnp.int32(0), jnp.int32(0), jnp.int32(ranks), jnp.int32(0)))
@@ -560,12 +563,16 @@
         part = pl.ds(index * step_rows, step_rows)
         return pltpu.make_async_copy(tokens.at[part], out_hbm.at[part], out_sem.at[index])
 
-    for index in range(rows // step_rows):
-        span = slice(index * step_rows, (index + 1) * step_rows)
+    def finish(index, carry):
+        start = pl.multiple_of(index * LANES, LANES)
         for part in range(parts):
             cols = slice(part * LANES, (part + 1) * LANES)
-            moe = sums_of[pl.ds(parts + index * step_rows * parts + part, step_rows, stride=parts), :]
-            tokens[span, cols] = (base[span, cols] + moe).astype(BF16)
+            moe = sums_of[pl.ds(parts + start * parts + part, LANES, stride=parts), :]
+            tokens[pl.ds(start, LANES), cols] = (base[pl.ds(start, LANES), cols] + moe).astype(BF16)
+        return carry
+
+    for index in range(rows // step_rows):
+        lax.fori_loop(index * step_rows // LANES, (index + 1) * step_rows // LANES, finish, 0)
         store(index).start()
     for index in range(rows // step_rows):
         store(index).wait()
@@ -655,9 +662,9 @@
                 pltpu.VMEM((rows, width), BF16),
                 pltpu.VMEM((rows, width), F32),
                 *[pltpu.VMEM((rows + 1, parts, LANES), F32) for _ in range(2)],
+                pltpu.VMEM((TILE, parts, LANES), F32),
+                pltpu.VMEM((TILE, width), BF16),
                 staged,
-                pltpu.VMEM((TILE, width), BF16),
-                pltpu.VMEM((TILE, parts, LANES), F32),
                 *double,
                 *[pltpu.SemaphoreType.DMA(shape) for shape in ((5,), (2, 3), (4,))],
             ],

time: 352 us -> 337 us (0.957)
  the two profiles are of different devices: /device:TPU:107 before, /device:TPU:98 now
where the time goes in v5:
time: 337 us; the launch traced here: 336 us
  Pallas kernels  336 us (100%)
    pallas_call x1, Pallas kernels, local_program(): pl.pallas_call(functools.partial(fused_kernel, (rows, width, seq, hidden,...  273 us
    pallas_call x1, Pallas kernels, local_program(): pl.pallas_call(functools.partial(compact_kernel, (rows, width, STATIC, la...  62.8 us

profile of v5, /device:TPU:98, one launch (start us, length us, event | category | flops | bytes accessed | tf_op | source)
XLA Modules:
  0.0 336.4 jit_solution(11880180948185850853)
XLA Ops:
  0.0 273.4 %shard_map.163 = (f32[2048,1024]{1,0:T(8,128)}, bf16[2048,1024]{1,0:T(8,128)(2,1)}, s32[150,128]{1,0:T(8,128)}, f32[150,128]{1,0:T(8,128)}, s32[8,128]{1,0:T(8,1...) custom-call(bf16[2048,1024]{1,0:T(8,128)(2,1)} %bitcast.22, ...), custom_call_target="tpu_custom_call" | custom-call | flops 270582939648 | bytes 100663296 | tf_op jit(solution)/shard_map/pallas_call | solution.py:620
  273.4 62.8 %shard_map.164 = bf16[2048,1024]{1,0:T(8,128)(2,1)} custom-call(s32[19200]{0:T(1024)} %bitcast.21, f32[150,128]{1,0:T(8,128)} %get-tuple-element.14.shares_hbm, s32[8,128]{1,0:T(8,128)} %get-tuple-element.15.counts_hbm, bf16[2048,1024]{1,0:T(8,128)(2,1)} %get-tuple-element.16.tokens_hbm, f32[2048,1024]{1,0:T(8,128)} %get-tuple-element.17.base_hbm, ...), custom_call_target="tpu_custom_call" | custom-call | tf_op jit(solution)/shard_map/pallas_call | solution.py:653
